TPU v7x, 8 devices: a whole 2x2x1 slice. The times are simulated.
8 devices in a mesh: data: 8 (over z, y, x, core).
Axes of the slice: x: 2, y: 2, z: 1, core: 2. Of those that a mesh axis runs over, the one named last changes fastest.
Arguments:
- z_one: bfloat16 [1024, 128], P('data')
- z_two: bfloat16 [1024, 128], P('data')
- protos: bfloat16 [1000, 128], replicated
- queue_one: bfloat16 [4096, 128], P('data')
- queue_two: bfloat16 [4096, 128], P('data')
Outputs:
- output 1: float32 [1024, 1000], P('data')
- output 2: float32 [1024, 1000], P('data')
- output 3: float32 [], replicated
- output 4: float32 [1024, 128], P('data')
- output 5: float32 [1024, 128], P('data')
- output 6: float32 [1000, 128], replicated
All inputs are finite; a program needn't handle non-finite values.
Results may differ from a plain program's by a relative error of at most 0.001.
Values are sent between devices in bfloat16 or wider.
A program may use at most 1 GiB of HBM per device.

v0:
```python
import jax
import jax.numpy as jnp
from jax import lax
from jax.sharding import PartitionSpec as P

EPSILON = 0.05
value_a11 = 0.1
value_a14 = 3


def view_codes(own_rows, protos, batch_rows, total_rows):
    protos_count = protos.shape[0]
    scores = jnp.einsum("nd,kd->nk", own_rows, protos, preferred_element_type=jnp.float32)
    transport = jnp.exp(scores / EPSILON)
    for _ in range(value_a14 - 1):
        col_sum = lax.psum(jnp.sum(transport, axis=0), "data")
        transport = transport / (protos_count * col_sum)
        transport = transport / (total_rows * jnp.sum(transport, axis=1, keepdims=True))
    col_sum = lax.psum(jnp.sum(transport, axis=0), "data")
    plan_batch = transport[:batch_rows] / (protos_count * col_sum)
    return plan_batch / jnp.sum(plan_batch, axis=1, keepdims=True), scores[:batch_rows]


def solution(mesh):
    group_size = mesh.shape["data"]

    def local_step(z_one, z_two, protos, queue_one, queue_two):
        batch_rows = z_one.shape[0]
        total_rows = group_size * (batch_rows + queue_one.shape[0])
        batch_total = group_size * batch_rows
        codes_one, score_one = view_codes(jnp.concatenate([z_one, queue_one], axis=0), protos, batch_rows, total_rows)
        codes_two, score_two = view_codes(jnp.concatenate([z_two, queue_two], axis=0), protos, batch_rows, total_rows)
        logp_one = jax.nn.log_softmax(score_one / value_a11, axis=1)
        logp_two = jax.nn.log_softmax(score_two / value_a11, axis=1)
        part_loss = jnp.sum(codes_two * logp_one) + jnp.sum(codes_one * logp_two)
        swap_loss = -lax.psum(part_loss, "data") / (2 * batch_total)
        grad_coef = 1.0 / (2 * batch_total * value_a11)
        grad_s_one = ((jnp.exp(logp_one) - codes_two) * grad_coef).astype(jnp.bfloat16)
        grad_s_two = ((jnp.exp(logp_two) - codes_one) * grad_coef).astype(jnp.bfloat16)
        dz_one = jnp.einsum("nk,kd->nd", grad_s_one, protos, preferred_element_type=jnp.float32)
        dz_two = jnp.einsum("nk,kd->nd", grad_s_two, protos, preferred_element_type=jnp.float32)
        proto_part = jnp.einsum("nk,nd->kd", grad_s_one, z_one, preferred_element_type=jnp.float32) + jnp.einsum("nk,nd->kd", grad_s_two, z_two, preferred_element_type=jnp.float32)
        grad_protos = lax.psum(proto_part, "data")
        return codes_one, codes_two, swap_loss, dz_one, dz_two, grad_protos

    row_spec = P("data", None)
    full_spec = P(None, None)
    return jax.shard_map(
        local_step,
        mesh=mesh,
        in_specs=(row_spec, row_spec, full_spec, row_spec, row_spec),
        out_specs=(row_spec, row_spec, P(), row_spec, row_spec, full_spec),
        check_vma=False,
    )
```

profile of v0, /device:TPU:0, one launch (start us, length us, event | category | flops | bytes accessed | tf_op | source)
XLA Modules:
  0.0 159.9 jit_solution(17194544050988444396)
XLA Ops:
  7.2 0.0 copy-start
  7.2 0.0 copy-start.3
  7.2 0.0 copy-start.5
  7.2 0.0 all-reduce.5.cloned.1.call-start
  7.2 0.9 copy-done
  8.1 3.0 %fusion.11 = (f32[1000]{0:T(1024)S(1)}, f32[640,1000]{0,1:T(8,128)}) fusion(bf16[1000,128]{1,0:T(8,128)(2,1)S(1)} %copy-done, bf16[512,128]{1,0:T(8,128)(2,1)} %param.10, bf16[128,128]{1,0:T(8,128)(2,1)} %param.7), kind=kOutput, calls=%fused_computation.19 | convolution fusion | flops 165446688 | bytes 2983840 | tf_op jit(solution)/shard_map/nd,kd->nk/dot_general | solution.py:13
  11.1 0.0 copy-done.3
  11.1 0.0 copy-done.5
  11.1 0.7 fusion.10
  11.8 25.2 %all-reduce.2 = (f32[1000]{0:T(1024)S(1)}, f32[1000]{0:T(1024)S(1)}) all-reduce(f32[1000]{0:T(1024)S(1)} %get-tuple-element.21, f32[1000]{0:T(1024)S(1)} %get-tuple-element.23), channel_id=1, replica_groups=mesh['data'=8] {'data'}, use_global_device_ids=true, to_apply=%region_1.0 | all-reduce | flops 2000 | bytes 16000 | tf_op jit(solution)/shard_map/psum | solution.py:16
  37.0 0.0 copy-start.1
  37.0 1.3 fusion.14
  38.3 2.3 %divide_reduce_fusion = f32[640]{0:T(1024)S(1)} fusion(f32[640,1000]{0,1:T(8,128)} %get-tuple-element.24, f32[1000]{0:T(1024)S(1)} %broadcast_multiply_fusion.6), kind=kLoop, calls=%fused_computation.12 | loop fusion | flops 1919360 | bytes 2566560 | tf_op jit(solution)/shard_map/reduce_sum | solution.py:18
  40.6 0.0 copy-done.1
  40.6 0.9 fusion.7
  41.6 0.1 fusion.12
  41.7 0.5 divide_reduce_fusion.1
  42.2 0.9 fusion.6
  43.1 23.1 %all-reduce.1 = (f32[1000]{0:T(1024)S(1)}, f32[1000]{0:T(1024)S(1)}) all-reduce(f32[1000]{0:T(1024)S(1)} %fusion.6, f32[1000]{0:T(1024)S(1)} %fusion.7), channel_id=1, replica_groups=mesh['data'=8] {'data'}, use_global_device_ids=true, to_apply=%region_4.0 | all-reduce | flops 2000 | bytes 16000 | tf_op jit(solution)/shard_map/psum | solution.py:16
  66.3 0.0 copy-start.2
  66.3 0.7 fusion.9
  67.0 1.0 copy-done.2
  68.0 0.7 fusion.8
  68.7 3.4 %fusion.26 = (f32[1000]{0:T(1024)S(1)}, f32[640,1000]{0,1:T(8,128)}, f32[1000]{0:T(1024)S(1)}, f32[640,1000]{0,1:T(8,128)}) fusion(f32[640]{0:T(1024)S(1)} %broadcast_multiply_fusion, f32[1000]{0:T(1024)S(1)} %broadcast_multiply_fusion.5, f32[640]{0:T(1024)S(1)} %broadcast_multiply_fusion.1, f32[1000]{0:T(1024)S(1)} %broadcast_multiply_fusion.6, ...), kind=kLoop, calls=%fused_computation.57 | loop fusion | flops 7678000 | bytes 10274240 | tf_op jit(solution)/shard_map/reduce_sum | solution.py:19
  72.2 24.0 %all-reduce = (f32[1000]{0:T(1024)S(1)}, f32[1000]{0:T(1024)S(1)}) all-reduce(f32[1000]{0:T(1024)S(1)} %get-tuple-element.25, f32[1000]{0:T(1024)S(1)} %get-tuple-element.17), channel_id=1, replica_groups=mesh['data'=8] {'data'}, use_global_device_ids=true, to_apply=%region_7.0 | all-reduce | flops 2000 | bytes 16000 | tf_op jit(solution)/shard_map/psum | solution.py:19
  96.2 0.2 exponential_reduce_fusion.1
  96.4 1.3 divide_reduce_fusion.2
  97.6 0.0 copy-start.4
  97.6 2.0 %multiply_convert_fusion.1 = (bf16[128,1000]{0,1:T(8,128)(2,1)S(1)}, f32[128,1000]{0,1:T(8,128)}) fusion(f32[640,1000]{0,1:T(8,128)S(1)} %get-tuple-element.22, f32[128]{0:T(128)S(1)} %log.9, f32[128]{0:T(128)S(1)} %fusion.12, f32[128]{0:T(128)S(1)} %divide_reduce_fusion.2, f32[1000]{0:T(1024)S(1)} %broadcast_multiply_fusion.4, f32[640,1000]{0,1:T(8,128)} %get-tuple-element.18), kind=kLoop, calls=%fused_computation.26 | loop fusion | flops 1024000 | bytes 1797536 | tf_op jit(solution)/shard_map/convert_element_type | solution.py:38
  99.7 0.3 fusion.32
  100.0 1.2 exponential_reduce_fusion
  101.2 1.3 divide_reduce_fusion.3
  102.4 2.2 %multiply_convert_fusion = (bf16[128,1000]{0,1:T(8,128)(2,1)S(1)}, f32[128,1000]{0,1:T(8,128)}) fusion(f32[640,1000]{0,1:T(8,128)} %get-tuple-element.24, f32[128]{0:T(128)S(1)} %log.10, f32[128]{0:T(128)S(1)} %fusion.14, f32[128]{0:T(128)S(1)} %divide_reduce_fusion.3, f32[1000]{0:T(1024)S(1)} %broadcast_multiply_fusion.7, f32[640,1000]{0,1:T(8,128)} %get-tuple-element.26), kind=kLoop, calls=%fused_computation.25 | loop fusion | flops 1024000 | bytes 1797536 | tf_op jit(solution)/shard_map/convert_element_type | solution.py:39
  104.6 0.0 copy-done.4
  104.6 1.1 convolution_add_fusion
  105.7 0.0 all-reduce.5.cloned.1.call-update
  105.7 1.9 %multiply_reduce_fusion = f32[]{:T(128)} fusion(f32[128,1000]{0,1:T(8,128)} %get-tuple-element.27, f32[640,1000]{0,1:T(8,128)} %get-tuple-element.24, f32[128]{0:T(128)S(1)} %log.10, f32[128]{0:T(128)S(1)} %fusion.14), kind=kLoop, calls=%fused_computation.27 | loop fusion | flops 639999 | bytes 1025028 | tf_op jit(solution)/shard_map/reduce_sum | solution.py:35
  107.7 1.8 %multiply_reduce_fusion.1 = f32[]{:T(128)} fusion(f32[128,1000]{0,1:T(8,128)} %get-tuple-element.28, f32[640,1000]{0,1:T(8,128)S(1)} %get-tuple-element.22, f32[128]{0:T(128)S(1)} %log.9, f32[128]{0:T(128)S(1)} %fusion.12), kind=kLoop, calls=%fused_computation.28 | loop fusion | flops 639999 | bytes 1025028 | tf_op jit(solution)/shard_map/reduce_sum | solution.py:35
  110.7 0.9 fusion.30
  111.6 23.0 %psum.62 = f32[]{:T(128)} all-reduce(f32[]{:T(128)S(6)} %add.22), channel_id=1, replica_groups=mesh['data'=8] {'data'}, use_global_device_ids=true, to_apply=%region_22.0 | all-reduce | flops 1 | bytes 8 | tf_op jit(solution)/shard_map/psum | solution.py:36
  135.3 0.9 fusion.31
  136.2 13.9 %all-reduce.5.cloned.1.call-done = f32[1000,128]{1,0:T(8,128)} async-done(((f32[1000,128]{1,0:T(8,128)}), f32[1000,128]{1,0:T(8,128)}) %all-reduce.5.cloned.1.call-update) | async-done | bytes 512016 | tf_op jit(solution)/shard_map/psum | solution.py:43
  150.1 1.9 %copy.12 = f32[1000,128]{1,0:T(8,128)} copy(f32[1000,128]{1,0:T(8,128)} %all-reduce.5.cloned.1.call-done) | data formatting | bytes 1024000
  (12 shorter events, 0.0 us)
Async XLA Ops:
  7.2 1.0 copy-start
  7.2 3.9 %copy-start.3 = (bf16[128,128]{1,0:T(8,128)(2,1)S(1)}, bf16[128,128]{1,0:T(8,128)(2,1)}, u32[]{:S(2)}) copy-start(bf16[128,128]{1,0:T(8,128)(2,1)} %param.6) | copy-start | bytes 98308
  7.2 3.9 %copy-start.5 = (bf16[512,128]{1,0:T(8,128)(2,1)S(1)}, bf16[512,128]{1,0:T(8,128)(2,1)}, u32[]{:S(2)}) copy-start(bf16[512,128]{1,0:T(8,128)(2,1)} %param.9) | copy-start | bytes 393220
  7.2 142.9 %all-reduce.5.cloned.1.call-start = ((), (), s32[]{:S(2)}) async-start(), calls=%async_computation | async-start | bytes 1024000 | tf_op jit(solution)/shard_map/psum | solution.py:43
  37.0 3.6 %copy-start.1 = (f32[640,1000]{0,1:T(8,128)S(1)}, f32[640,1000]{0,1:T(8,128)}, u32[]{:S(2)}) copy-start(f32[640,1000]{0,1:T(8,128)} %get-tuple-element.24) | copy-start | bytes 7680004
  66.3 1.7 %copy-start.2 = (f32[640,1000]{0,1:T(8,128)S(1)}, f32[640,1000]{0,1:T(8,128)}, u32[]{:S(2)}) copy-start(f32[640,1000]{0,1:T(8,128)} %get-tuple-element.24) | copy-start | bytes 7680004
  97.6 7.0 %copy-start.4 = (bf16[128,128]{1,0:T(8,128)(2,1)S(1)}, bf16[128,128]{1,0:T(8,128)(2,1)}, u32[]{:S(2)}) copy-start(bf16[128,128]{1,0:T(8,128)(2,1)} %param.7) | copy-start | bytes 98308
Sparse Core Ops, SparseCore 0:
  105.8 44.1 all-reduce.4
where the time goes:
time: 161 us; the launch traced here: 160 us
  blocking collectives  95.3 us (59%)
  other arithmetic  22.8 us (14%)
  between operations  17.3 us (11%)
  waiting for transfers between devices  13.9 us (9%)
  matrix products  6.82 us (4%)
  local copies, waits for them, and re-layouts  3.75 us (2%)
    psum x3, blocking collectives, view_codes(): col_sum = lax.psum(jnp.sum(transport, axis=0), 'data')  72.4 us
    psum x1, blocking collectives, local_step(): swap_loss = -lax.psum(part_loss, 'data') / (2 * batch_total)  23 us
    psum x1, waiting for transfers between devices, local_step(): grad_protos = lax.psum(proto_part, 'data')  13.9 us
    reduce_sum x3, other arithmetic, view_codes(): col_sum = lax.psum(jnp.sum(transport, axis=0), 'data')  5.29 us
    reduce_sum x4, other arithmetic, view_codes(): jnp.sum(transport, axis=1, keepdims=True)  4.17 us
    unnamed x13, local copies, waits for them, and re-layouts  3.74 us
    reduce_sum x2, other arithmetic, local_step(): part_loss = jnp.sum(codes_two * logp_one) + jnp.sum(codes_one * logp_two)  3.72 us
    dot_general x2, matrix products, view_codes(): jnp.einsum('nd,kd->nk', own_rows, protos, preferred_element_type=jnp.floa...  3.68 us
  transfers between devices with their start and end apart: 1, of which 1 were waited for; matrix products, arithmetic and copies ran while one was open for 3% of the time, Pallas kernels for 0%

commit v1 on v0

v1 whole, which is shorter than its diff:
```python
import functools
import math

import jax
import jax.numpy as jnp
from jax import lax
from jax.experimental import pallas as pl
from jax.experimental.pallas import tpu as pltpu
from jax.sharding import PartitionSpec as P

EPSILON = 0.05
TEMPERATURE = 0.1
ROUNDS = 3
LANES = 128
MESH = pl.DeviceIdType.MESH
F32 = jnp.float32
BF16 = jnp.bfloat16
NT = (((1,), (1,)), ((), ()))


def kernel(
    n, protos, batch, queue,
    z1_hbm, z2_hbm, c_hbm, q1_hbm, q2_hbm,
    codes1_hbm, codes2_hbm, loss_ref, dz1_hbm, dz2_hbm, gp_hbm,
    craw, cpad, zall, qbuf, zt, atr, aall, pall, s10, lse, gbuf, gacc, wbuf, cpart, csum, lossx,
    codes, dz, gp,
    in_sem, out_sem, send_sem, recv_sem, zsend_sem, zrecv_sem, lsend_sem, lrecv_sem,
):
    tiles = cpad.shape[0] // LANES
    rows = batch + queue
    total_rows = n * rows
    batch_total = n * batch
    coef = 1.0 / (2 * batch_total * TEMPERATURE)
    scale10 = math.log2(math.e) / TEMPERATURE

    me = lax.axis_index("data")
    bit0 = lax.rem(me, 2)
    bit1 = lax.rem(me // 2, 2)
    bit2 = me // 4

    def peer(k):
        b0, b1, b2 = k % 2, (k // 2) % 2, k // 4
        return (lax.rem(bit2 + b2, 2) * 2 + lax.rem(bit1 + b1, 2)) * 2 + lax.rem(bit0 + b0, 2)

    far_first = (6, 7, 4, 5, 2, 3, 1)

    c_in = pltpu.make_async_copy(c_hbm, craw, in_sem.at[0])
    z_in = [pltpu.make_async_copy(h, zall.at[me, v], in_sem.at[1 + v]) for v, h in enumerate((z1_hbm, z2_hbm))]
    q_in = [pltpu.make_async_copy(h, qbuf.at[v], in_sem.at[3 + v]) for v, h in enumerate((q1_hbm, q2_hbm))]
    c_in.start()
    z_in[0].start()
    q_in[0].start()
    z_in[1].start()
    q_in[1].start()

    barrier = pltpu.get_barrier_semaphore()
    for k in far_first:
        pl.semaphore_signal(barrier, inc=1, device_id=(peer(k),), device_id_type=MESH)

    c_in.wait()
    cpad[pl.ds(protos // 16 * 16, cpad.shape[0] - protos // 16 * 16), :] = jnp.zeros(
        (cpad.shape[0] - protos // 16 * 16, LANES), BF16)
    cpad[pl.ds(0, protos), :] = craw[...]

    lane = lax.broadcasted_iota(jnp.int32, (1, LANES), 1)
    tail_ok = lane < (protos - (tiles - 1) * LANES)
    tail_mask = tail_ok.astype(F32)

    def fold(x):
        return jnp.sum(x.reshape(x.shape[0] // 8, 8, LANES), axis=0)

    def publish(t, v, acc):
        for j in range(tiles):
            cpart[v, pl.ds(8 * j, 8), :] = acc[j]
        out = cpart[v, pl.ds(0, tiles, stride=8), :]
        for s in range(1, 8):
            out = out + cpart[v, pl.ds(s, tiles, stride=8), :]
        csum[t, v, me] = out

    def sum_copy(t, v, k):
        return pltpu.make_async_remote_copy(
            src_ref=csum.at[t, v, me], dst_ref=csum.at[t, v, me],
            send_sem=send_sem.at[t, v, k - 1], recv_sem=recv_sem.at[t, v, k - 1],
            device_id=(peer(k),), device_id_type=MESH)

    def send_sums(t, v):
        for k in far_first:
            sum_copy(t, v, k).start()

    def col_scale(t, v):
        for k in far_first:
            sum_copy(t, v, k).wait_recv()
        c = csum[t, v, 0]
        for d in range(1, n):
            c = c + csum[t, v, d]
        w = 1.0 / (protos * c)
        index = (lax.broadcasted_iota(jnp.int32, (tiles, LANES), 0) * LANES
                 + lax.broadcasted_iota(jnp.int32, (tiles, LANES), 1))
        wbuf[v] = jnp.where(index < protos, w, 0.0)

    def first_pass(v):
        acc = [jnp.zeros((8, LANES), F32) for _ in range(tiles)]
        blocks = [(zall.at[me, v], 0, batch)]
        step = queue // 2
        blocks += [(qbuf.at[v, pl.ds(i * step, step)], batch + i * step, step) for i in range(2)]
        for ref, start, size in blocks:
            x = ref[...]
            for jj in range(tiles // 2):
                s = lax.dot_general(x, cpad[pl.ds(jj * 256, 256), :], NT, preferred_element_type=F32)
                for h in range(2):
                    e = jnp.exp2(s[:, h * LANES:(h + 1) * LANES] * scale10)
                    a = e * e
                    atr[v, 2 * jj + h, pl.ds(start, size), :] = a
                    acc[2 * jj + h] = acc[2 * jj + h] + fold(a)
        return acc

    def sink_pass(v):
        acc = [jnp.zeros((8, LANES), F32) for _ in range(tiles)]
        step = 128
        for b in range(rows // step):
            sl = pl.ds(b * step, step)
            p = atr[v, 0, sl, :] * wbuf[v, 0:1, :]
            for j in range(1, tiles):
                p = p + atr[v, j, sl, :] * wbuf[v, j:j + 1, :]
            u = 1.0 / (total_rows * jnp.sum(p, axis=1, keepdims=True))
            for j in range(tiles):
                acc[j] = acc[j] + fold(atr[v, j, sl, :] * u)
        return acc

    z_in[0].wait()
    q_in[0].wait()
    publish(0, 0, first_pass(0))
    pl.semaphore_wait(barrier, n - 1)
    send_sums(0, 0)
    z_in[1].wait()
    q_in[1].wait()
    publish(0, 1, first_pass(1))
    send_sums(0, 1)

    def z_copy(k, owner):
        return pltpu.make_async_remote_copy(
            src_ref=zall.at[owner], dst_ref=zall.at[owner],
            send_sem=zsend_sem.at[k - 1], recv_sem=zrecv_sem.at[k - 1],
            device_id=(peer(k if k in (1, 2, 4, 6) else 1),), device_id_type=MESH)

    for k in (6, 2, 4, 1):
        z_copy(k, me).start()

    def relay(k):
        z_copy(k, me).wait_recv()
        z_copy(k + 1, peer(k)).start()

    def prepare(k):
        d = peer(k)
        if k in (3, 5, 7, 1):
            z_copy(k, me).wait_recv()
        sl = pl.ds(pl.multiple_of(d * batch, batch), batch)
        x = zall[d].reshape(2 * batch, LANES)
        for v in range(2):
            zt[v, :, sl] = zall[d, v].T
        p = None
        for jj in range(tiles // 2):
            s = lax.dot_general(x, cpad[pl.ds(jj * 256, 256), :], NT, preferred_element_type=F32)
            for h in range(2):
                j = 2 * jj + h
                sj = s[:, h * LANES:(h + 1) * LANES]
                e = jnp.exp2(sj * scale10)
                if j == tiles - 1:
                    e = e * tail_mask
                a = e * e
                for v in range(2):
                    half = slice(v * batch, (v + 1) * batch)
                    aall[v, j, sl, :] = a[half]
                    pall[v, j, sl, :] = e[half]
                    if k == 0:
                        s10[v, j] = sj[half] * (1.0 / TEMPERATURE)
                p = e if p is None else p + e
        r = jnp.sum(p, axis=1, keepdims=True)
        inv = coef / r
        if k == 0:
            log_r = jnp.log(r)
            for v in range(2):
                lse[v] = jnp.broadcast_to(log_r[v * batch:(v + 1) * batch], (batch, LANES))
        for v in range(2):
            for j in range(tiles):
                pall[v, j, sl, :] = pall[v, j, sl, :] * inv[v * batch:(v + 1) * batch]

    prepare(0)
    for v in range(2):
        col_scale(0, v)
        publish(1, v, sink_pass(v))
        send_sums(1, v)

    for k in (2, 4, 6):
        relay(k)
    for k in (1, 2, 4):
        prepare(k)
    for v in range(2):
        col_scale(1, v)
        publish(2, v, sink_pass(v))
        send_sums(2, v)
    for k in (6, 3, 5, 7):
        prepare(k)

    own = pl.ds(pl.multiple_of(me * batch, batch), batch)

    def own_codes(v):
        p = None
        for j in range(tiles):
            t = aall[v, j, own, :] * wbuf[v, j:j + 1, :]
            p = t if p is None else p + t
        inv = 1.0 / jnp.sum(p, axis=1, keepdims=True)
        part = jnp.zeros((8, LANES), F32)
        for j in range(tiles):
            q = aall[v, j, own, :] * wbuf[v, j:j + 1, :] * inv
            width = min(LANES, protos - j * LANES)
            codes[v, :, j * LANES:j * LANES + width] = q[:, :width]
            part = part + fold(q * (s10[1 - v, j] - lse[1 - v]))
        return part

    def final_pass(v):
        for d in range(n):
            sl = pl.ds(d * batch, batch)
            p = None
            for j in range(tiles):
                t = aall[v, j, sl, :] * wbuf[v, j:j + 1, :]
                p = t if p is None else p + t
            q = coef / jnp.sum(p, axis=1, keepdims=True)
            for j in range(tiles):
                g = pall[1 - v, j, sl, :] - aall[v, j, sl, :] * wbuf[v, j:j + 1, :] * q
                gbuf[1 - v, j // 2, sl, (j % 2) * LANES:(j % 2 + 1) * LANES] = g.astype(BF16)

    loss_part = []
    outs = []

    def out(src, dst, i):
        copy = pltpu.make_async_copy(src, dst, out_sem.at[i])
        copy.start()
        outs.append(copy)

    def finish(v):
        col_scale(2, v)
        loss_part.append(own_codes(v))
        out(codes.at[v], (codes1_hbm, codes2_hbm)[v], v)

    def loss_copy(k):
        return pltpu.make_async_remote_copy(
            src_ref=lossx.at[me], dst_ref=lossx.at[me],
            send_sem=lsend_sem.at[k - 1], recv_sem=lrecv_sem.at[k - 1],
            device_id=(peer(k),), device_id_type=MESH)

    def dz_of(v):
        o = None
        for jj in range(tiles // 2):
            t = jnp.dot(gbuf[v, jj, own, :], cpad[pl.ds(jj * 256, 256), :], preferred_element_type=F32)
            o = t if o is None else o + t
        dz[v] = o
        out(dz.at[v], (dz1_hbm, dz2_hbm)[v], 2 + v)

    finish(0)
    final_pass(0)
    for jj in range(tiles // 2):
        gacc[jj] = jnp.dot(zt[1], gbuf[1, jj], preferred_element_type=F32)
    dz_of(1)
    finish(1)
    lossx[me] = loss_part[0] + loss_part[1]
    for k in far_first:
        loss_copy(k).start()
    final_pass(1)
    for jj in range(tiles // 2):
        g = gacc[jj] + jnp.dot(zt[0], gbuf[0, jj], preferred_element_type=F32)
        size = min(256, protos - jj * 256)
        gp[pl.ds(jj * 256, size), :] = g.T[:size]
    out(gp, gp_hbm, 4)
    dz_of(0)

    for k in far_first:
        loss_copy(k).wait_recv()
    acc = lossx[0]
    for d in range(1, n):
        acc = acc + lossx[d]
    loss_ref[0, 0] = jnp.sum(acc) * (-1.0 / (2 * batch_total))

    for t in range(ROUNDS):
        for v in range(2):
            for k in far_first:
                sum_copy(t, v, k).wait_send()
    for k in range(1, n):
        z_copy(k, me).wait_send()
        loss_copy(k).wait_send()
    for copy in outs:
        copy.wait()


def solution(mesh):
    n = mesh.shape["data"]

    def local_step(z_one, z_two, protos, queue_one, queue_two):
        k, width = protos.shape
        batch, queue = z_one.shape[0], queue_one.shape[0]
        rows = batch + queue
        pad = (k + 255) // 256 * 256
        tiles = pad // LANES
        anywhere = pl.BlockSpec(memory_space=pl.ANY)
        sem = pltpu.SemaphoreType.DMA
        outs = pl.pallas_call(
            functools.partial(kernel, n, k, batch, queue),
            out_shape=(
                jax.ShapeDtypeStruct((batch, k), F32),
                jax.ShapeDtypeStruct((batch, k), F32),
                jax.ShapeDtypeStruct((1, 1), F32),
                jax.ShapeDtypeStruct((batch, width), F32),
                jax.ShapeDtypeStruct((batch, width), F32),
                jax.ShapeDtypeStruct((k, width), F32),
            ),
            in_specs=[anywhere] * 5,
            out_specs=(anywhere, anywhere, pl.BlockSpec(memory_space=pltpu.SMEM), anywhere, anywhere, anywhere),
            scratch_shapes=[
                pltpu.VMEM((k, width), BF16),
                pltpu.VMEM((pad, width), BF16),
                pltpu.VMEM((n, 2, batch, width), BF16),
                pltpu.VMEM((2, queue, width), BF16),
                pltpu.VMEM((2, width, n * batch), BF16),
                pltpu.VMEM((2, tiles, rows, LANES), F32),
                pltpu.VMEM((2, tiles, n * batch, LANES), F32),
                pltpu.VMEM((2, tiles, n * batch, LANES), F32),
                pltpu.VMEM((2, tiles, batch, LANES), F32),
                pltpu.VMEM((2, batch, LANES), F32),
                pltpu.VMEM((2, tiles // 2, n * batch, 256), BF16),
                pltpu.VMEM((tiles // 2, width, 256), F32),
                pltpu.VMEM((2, tiles, LANES), F32),
                pltpu.VMEM((2, 8 * tiles, LANES), F32),
                pltpu.VMEM((ROUNDS, 2, n, tiles, LANES), F32),
                pltpu.VMEM((n, 8, LANES), F32),
                pltpu.VMEM((2, batch, k), F32),
                pltpu.VMEM((2, batch, width), F32),
                pltpu.VMEM((k, width), F32),
                sem((5,)),
                sem((5,)),
                sem((ROUNDS, 2, n - 1)),
                sem((ROUNDS, 2, n - 1)),
                sem((n - 1,)),
                sem((n - 1,)),
                sem((n - 1,)),
                sem((n - 1,)),
            ],
            compiler_params=pltpu.CompilerParams(collective_id=0, has_side_effects=True),
        )(z_one, z_two, protos, queue_one, queue_two)
        codes_one, codes_two, loss, dz_one, dz_two, grad_protos = outs
        return codes_one, codes_two, loss[0, 0], dz_one, dz_two, grad_protos

    row_spec = P("data", None)
    full_spec = P(None, None)
    return jax.shard_map(
        local_step,
        mesh=mesh,
        in_specs=(row_spec, row_spec, full_spec, row_spec, row_spec),
        out_specs=(row_spec, row_spec, P(), row_spec, row_spec, full_spec),
        check_vma=False,
    )
```

time: 161 us -> 29.3 us (0.18)
  blocking collectives: 95.3 us -> 0 us
  other arithmetic: 22.8 us -> 0 us
  Pallas kernels: 0 us -> 21.4 us
  between operations: 17.3 us -> 2.41 us
  waiting for transfers between devices: 13.9 us -> 0 us
  matrix products: 6.82 us -> 0 us
    psum x4 -> x0, blocking collectives: 95.3 us -> none  [the longest x3 72.4 us: view_codes(): col_sum = lax.psum(jnp.sum(transport, axis=0), 'data')]
    pallas_call x0 -> x1, Pallas kernels: none -> 21.4 us  [local_step(): pl.pallas_call(functools.partial(kernel, n, k, batch, queue), out_shape=(...]
    reduce_sum x13 -> x0, other arithmetic: 17 us -> none  [the longest x3 5.29 us: view_codes(): col_sum = lax.psum(jnp.sum(transport, axis=0), 'data')]
    psum x1 -> x0, waiting for transfers between devices: 13.9 us -> none  [local_step(): grad_protos = lax.psum(proto_part, 'data')]
    dot_general x6 -> x0, matrix products: 6.82 us -> none  [the longest x2 3.68 us: view_codes(): jnp.einsum('nd,kd->nk', own_rows, protos, preferred_element_type=jnp.floa...]
    convert_element_type x2 -> x0, other arithmetic: 4.25 us -> none  [the longest x1 2.2 us: local_step(): ((jnp.exp(logp_two) - codes_one) * grad_coef).astype(jnp.bfloat16)]
  transfers between devices with their start and end apart: 1 -> 0, of which waited for: 1 -> 0; matrix products, arithmetic and copies ran while one was open for 3% -> 0% of each run, Pallas kernels for 0% -> 0%
where the time goes in v1:
time: 29.3 us; the launch traced here: 29.1 us
  Pallas kernels  21.4 us (73%)
  local copies, waits for them, and re-layouts  5.33 us (18%)
  between operations  2.41 us (8%)
    pallas_call x1, Pallas kernels, local_step(): pl.pallas_call(functools.partial(kernel, n, k, batch, queue), out_shape=(...  21.4 us
    unnamed x13, local copies, waits for them, and re-layouts  5.33 us

profile of v1, /device:TPU:0, one launch (start us, length us, event | category | flops | bytes accessed | tf_op | source)
XLA Modules:
  0.0 29.1 jit_solution(17963064357153072592)
XLA Ops:
  0.6 21.4 %shard_map.100 = (f32[128,1000]{1,0:T(8,128)}, f32[128,1000]{1,0:T(8,128)}, f32[1,1]{1,0:T(1,128)}, f32[128,128]{1,0:T(8,128)}, f32[128,128]{1,0:T(8,128)}, /*index=5*/f32[1000,128]{1,0:T(8,128)}) custom-call(bf16[128,128]{1,0:T(8,128)(2,1)} %z1_hbm.1, bf16[128,128]{1,0:T(8,128)(2,1)} %z2_hbm.1, bf16[1000,128]{1,0:T(8,128)(2,1)} %c_hbm.1, ...), custom_call_target="tpu_custom_call" | custom-call | tf_op jit(solution)/shard_map/pallas_call | solution.py:306
  22.0 0.0 copy-start
  22.0 2.1 %copy.11 = f32[128,1000]{0,1:T(8,128)} copy(f32[128,1000]{1,0:T(8,128)} %get-tuple-element.18) | data formatting | bytes 1024000
  24.1 0.0 copy-done
  24.1 0.0 copy-start.3
  24.1 0.0 copy-start.1
  24.1 1.0 %copy.12 = f32[128,1000]{0,1:T(8,128)} copy(f32[128,1000]{1,0:T(8,128)S(1)} %copy-done) | data formatting | bytes 1024000
  25.7 0.0 copy-done.3
  25.7 0.0 copy-start.2
  25.8 0.6 %copy.18 = f32[128,128]{1,0:T(8,128)} copy(f32[128,128]{1,0:T(8,128)S(1)} %copy-done.3) | data formatting | bytes 131072
  26.4 0.2 copy-done.2
  26.6 0.6 %copy.19 = f32[128,128]{1,0:T(8,128)} copy(f32[128,128]{1,0:T(8,128)S(1)} %copy-done.2) | data formatting | bytes 131072
  27.2 0.0 copy-done.1
  27.2 0.8 %copy.20 = f32[1000,128]{1,0:T(8,128)} copy(f32[1000,128]{1,0:T(8,128)S(1)} %copy-done.1) | data formatting | bytes 1024000
Async XLA Ops:
  22.0 2.1 %copy-start = (f32[128,1000]{1,0:T(8,128)S(1)}, f32[128,1000]{1,0:T(8,128)}, u32[]{:S(2)}) copy-start(f32[128,1000]{1,0:T(8,128)} %get-tuple-element.19) | copy-start | bytes 1536004
  24.1 1.6 %copy-start.3 = (f32[128,128]{1,0:T(8,128)S(1)}, f32[128,128]{1,0:T(8,128)}, u32[]{:S(2)}) copy-start(f32[128,128]{1,0:T(8,128)} %get-tuple-element.33) | copy-start | bytes 196612
  24.1 3.1 %copy-start.1 = (f32[1000,128]{1,0:T(8,128)S(1)}, f32[1000,128]{1,0:T(8,128)}, u32[]{:S(2)}) copy-start(f32[1000,128]{1,0:T(8,128)} %get-tuple-element.35) | copy-start | bytes 1536004
  25.7 0.8 %copy-start.2 = (f32[128,128]{1,0:T(8,128)S(1)}, f32[128,128]{1,0:T(8,128)}, u32[]{:S(2)}) copy-start(f32[128,128]{1,0:T(8,128)} %get-tuple-element.34) | copy-start | bytes 196612

commit v2 on v1

--- a/solution.py
+++ b/solution.py
@@ -18,19 +18,17 @@
 NT = (((1,), (1,)), ((), ()))
 
 
-def kernel(
+def sums_kernel(
     n, protos, batch, queue,
     z1_hbm, z2_hbm, c_hbm, q1_hbm, q2_hbm,
-    codes1_hbm, codes2_hbm, loss_ref, dz1_hbm, dz2_hbm, gp_hbm,
-    craw, cpad, zall, qbuf, zt, atr, aall, pall, s10, lse, gbuf, gacc, wbuf, cpart, csum, lossx,
-    codes, dz, gp,
-    in_sem, out_sem, send_sem, recv_sem, zsend_sem, zrecv_sem, lsend_sem, lrecv_sem,
+    aall, pall, sall, zt, cpad, wbuf, lse_sum,
+    craw, zall, qbuf, atr, cpart, csum,
+    in_sem, send_sem, recv_sem, zsend_sem, zrecv_sem,
 ):
     tiles = cpad.shape[0] // LANES
     rows = batch + queue
     total_rows = n * rows
-    batch_total = n * batch
-    coef = 1.0 / (2 * batch_total * TEMPERATURE)
+    coef = 1.0 / (2 * n * batch * TEMPERATURE)
     scale10 = math.log2(math.e) / TEMPERATURE
 
     me = lax.axis_index("data")
@@ -172,15 +170,11 @@
                     half = slice(v * batch, (v + 1) * batch)
                     aall[v, j, sl, :] = a[half]
                     pall[v, j, sl, :] = e[half]
-                    if k == 0:
-                        s10[v, j] = sj[half] * (1.0 / TEMPERATURE)
+                    sall[v, j, sl, :] = sj[half]
                 p = e if p is None else p + e
         r = jnp.sum(p, axis=1, keepdims=True)
         inv = coef / r
-        if k == 0:
-            log_r = jnp.log(r)
-            for v in range(2):
-                lse[v] = jnp.broadcast_to(log_r[v * batch:(v + 1) * batch], (batch, LANES))
+        lse_sum[d] = fold(jnp.broadcast_to(jnp.log(r), (2 * batch, LANES)))
         for v in range(2):
             for j in range(tiles):
                 pall[v, j, sl, :] = pall[v, j, sl, :] * inv[v * batch:(v + 1) * batch]
@@ -202,7 +196,30 @@
     for k in (6, 3, 5, 7):
         prepare(k)
 
+    for v in range(2):
+        col_scale(2, v)
+    for t in range(ROUNDS):
+        for v in range(2):
+            for k in far_first:
+                sum_copy(t, v, k).wait_send()
+    for k in range(1, n):
+        z_copy(k, me).wait_send()
+
+
+def grads_kernel(
+    n, protos, batch,
+    aall, pall, sall, zt, cpad, wbuf, lse_sum,
+    codes1_hbm, codes2_hbm, loss_ref, dz1_hbm, dz2_hbm, gp_hbm,
+    gbuf, gacc, codes, dz, gp, out_sem,
+):
+    tiles = cpad.shape[0] // LANES
+    batch_total = n * batch
+    coef = 1.0 / (2 * batch_total * TEMPERATURE)
+    me = lax.axis_index("data")
     own = pl.ds(pl.multiple_of(me * batch, batch), batch)
+
+    def fold(x):
+        return jnp.sum(x.reshape(x.shape[0] // 8, 8, LANES), axis=0)
 
     def own_codes(v):
         p = None
@@ -210,44 +227,35 @@
             t = aall[v, j, own, :] * wbuf[v, j:j + 1, :]
             p = t if p is None else p + t
         inv = 1.0 / jnp.sum(p, axis=1, keepdims=True)
-        part = jnp.zeros((8, LANES), F32)
         for j in range(tiles):
             q = aall[v, j, own, :] * wbuf[v, j:j + 1, :] * inv
-            width = min(LANES, protos - j * LANES)
-            codes[v, :, j * LANES:j * LANES + width] = q[:, :width]
-            part = part + fold(q * (s10[1 - v, j] - lse[1 - v]))
-        return part
+            size = min(LANES, protos - j * LANES)
+            codes[v, pl.ds(j * LANES, size), :] = q.T[:size]
 
     def final_pass(v):
+        part = jnp.zeros((8, LANES), F32)
         for d in range(n):
             sl = pl.ds(d * batch, batch)
             p = None
+            m = None
             for j in range(tiles):
                 t = aall[v, j, sl, :] * wbuf[v, j:j + 1, :]
+                u = t * sall[1 - v, j, sl, :]
                 p = t if p is None else p + t
+                m = u if m is None else m + u
             q = coef / jnp.sum(p, axis=1, keepdims=True)
+            part = part + fold(m * q)
             for j in range(tiles):
                 g = pall[1 - v, j, sl, :] - aall[v, j, sl, :] * wbuf[v, j:j + 1, :] * q
                 gbuf[1 - v, j // 2, sl, (j % 2) * LANES:(j % 2 + 1) * LANES] = g.astype(BF16)
-
-    loss_part = []
+        return part
+
     outs = []
 
-    def out(src, dst, i):
-        copy = pltpu.make_async_copy(src, dst, out_sem.at[i])
+    def out(src, dst):
+        copy = pltpu.make_async_copy(src, dst, out_sem.at[len(outs)])
         copy.start()
         outs.append(copy)
-
-    def finish(v):
-        col_scale(2, v)
-        loss_part.append(own_codes(v))
-        out(codes.at[v], (codes1_hbm, codes2_hbm)[v], v)
-
-    def loss_copy(k):
-        return pltpu.make_async_remote_copy(
-            src_ref=lossx.at[me], dst_ref=lossx.at[me],
-            send_sem=lsend_sem.at[k - 1], recv_sem=lrecv_sem.at[k - 1],
-            device_id=(peer(k),), device_id_type=MESH)
 
     def dz_of(v):
         o = None
@@ -255,39 +263,29 @@
             t = jnp.dot(gbuf[v, jj, own, :], cpad[pl.ds(jj * 256, 256), :], preferred_element_type=F32)
             o = t if o is None else o + t
         dz[v] = o
-        out(dz.at[v], (dz1_hbm, dz2_hbm)[v], 2 + v)
-
-    finish(0)
-    final_pass(0)
+        out(dz.at[v], (dz1_hbm, dz2_hbm)[v])
+
+    own_codes(0)
+    out(codes.at[0], codes1_hbm)
+    own_codes(1)
+    out(codes.at[1], codes2_hbm)
+    part = final_pass(0)
     for jj in range(tiles // 2):
         gacc[jj] = jnp.dot(zt[1], gbuf[1, jj], preferred_element_type=F32)
     dz_of(1)
-    finish(1)
-    lossx[me] = loss_part[0] + loss_part[1]
-    for k in far_first:
-        loss_copy(k).start()
-    final_pass(1)
+    part = part + final_pass(1)
     for jj in range(tiles // 2):
         g = gacc[jj] + jnp.dot(zt[0], gbuf[0, jj], preferred_element_type=F32)
         size = min(256, protos - jj * 256)
         gp[pl.ds(jj * 256, size), :] = g.T[:size]
-    out(gp, gp_hbm, 4)
+    out(gp, gp_hbm)
     dz_of(0)
 
-    for k in far_first:
-        loss_copy(k).wait_recv()
-    acc = lossx[0]
+    logs = lse_sum[0]
     for d in range(1, n):
-        acc = acc + lossx[d]
-    loss_ref[0, 0] = jnp.sum(acc) * (-1.0 / (2 * batch_total))
-
-    for t in range(ROUNDS):
-        for v in range(2):
-            for k in far_first:
-                sum_copy(t, v, k).wait_send()
-    for k in range(1, n):
-        z_copy(k, me).wait_send()
-        loss_copy(k).wait_send()
+        logs = logs + lse_sum[d]
+    scaled = jnp.sum(part) / (coef * TEMPERATURE) - jnp.sum(logs) / LANES
+    loss_ref[0, 0] = scaled * (-1.0 / (2 * batch_total))
     for copy in outs:
         copy.wait()
 
@@ -303,51 +301,62 @@
         tiles = pad // LANES
         anywhere = pl.BlockSpec(memory_space=pl.ANY)
         sem = pltpu.SemaphoreType.DMA
-        outs = pl.pallas_call(
-            functools.partial(kernel, n, k, batch, queue),
+        vmem = pl.BlockSpec(memory_space=pltpu.VMEM)
+        whole = n * batch
+        shared = pl.pallas_call(
+            functools.partial(sums_kernel, n, k, batch, queue),
             out_shape=(
-                jax.ShapeDtypeStruct((batch, k), F32),
-                jax.ShapeDtypeStruct((batch, k), F32),
+                pltpu.VMEM((2, tiles, whole, LANES), F32),
+                pltpu.VMEM((2, tiles, whole, LANES), F32),
+                pltpu.VMEM((2, tiles, whole, LANES), F32),
+                pltpu.VMEM((2, width, whole), BF16),
+                pltpu.VMEM((pad, width), BF16),
+                pltpu.VMEM((2, tiles, LANES), F32),
+                pltpu.VMEM((n, 8, LANES), F32),
+            ),
+            in_specs=[pl.BlockSpec(memory_space=pltpu.HBM)] * 5,
+            out_specs=(vmem,) * 7,
+            scratch_shapes=[
+                pltpu.VMEM((k, width), BF16),
+                pltpu.VMEM((n, 2, batch, width), BF16),
+                pltpu.VMEM((2, queue, width), BF16),
+                pltpu.VMEM((2, tiles, rows, LANES), F32),
+                pltpu.VMEM((2, 8 * tiles, LANES), F32),
+                pltpu.VMEM((ROUNDS, 2, n, tiles, LANES), F32),
+                sem((5,)),
+                sem((ROUNDS, 2, n - 1)),
+                sem((ROUNDS, 2, n - 1)),
+                sem((n - 1,)),
+                sem((n - 1,)),
+            ],
+            compiler_params=pltpu.CompilerParams(
+                collective_id=0, has_side_effects=True, vmem_limit_bytes=14 << 20),
+            name="sums",
+        )(*(pltpu.with_memory_space_constraint(x, pltpu.HBM) for x in (z_one, z_two, protos, queue_one, queue_two)))
+        codes_one, codes_two, loss, dz_one, dz_two, grad_protos = pl.pallas_call(
+            functools.partial(grads_kernel, n, k, batch),
+            out_shape=(
+                jax.ShapeDtypeStruct((k, batch), F32),
+                jax.ShapeDtypeStruct((k, batch), F32),
                 jax.ShapeDtypeStruct((1, 1), F32),
                 jax.ShapeDtypeStruct((batch, width), F32),
                 jax.ShapeDtypeStruct((batch, width), F32),
                 jax.ShapeDtypeStruct((k, width), F32),
             ),
-            in_specs=[anywhere] * 5,
+            in_specs=[vmem] * 7,
             out_specs=(anywhere, anywhere, pl.BlockSpec(memory_space=pltpu.SMEM), anywhere, anywhere, anywhere),
             scratch_shapes=[
-                pltpu.VMEM((k, width), BF16),
-                pltpu.VMEM((pad, width), BF16),
-                pltpu.VMEM((n, 2, batch, width), BF16),
-                pltpu.VMEM((2, queue, width), BF16),
-                pltpu.VMEM((2, width, n * batch), BF16),
-                pltpu.VMEM((2, tiles, rows, LANES), F32),
-                pltpu.VMEM((2, tiles, n * batch, LANES), F32),
-                pltpu.VMEM((2, tiles, n * batch, LANES), F32),
-                pltpu.VMEM((2, tiles, batch, LANES), F32),
-                pltpu.VMEM((2, batch, LANES), F32),
-                pltpu.VMEM((2, tiles // 2, n * batch, 256), BF16),
+                pltpu.VMEM((2, tiles // 2, whole, 256), BF16),
                 pltpu.VMEM((tiles // 2, width, 256), F32),
-                pltpu.VMEM((2, tiles, LANES), F32),
-                pltpu.VMEM((2, 8 * tiles, LANES), F32),
-                pltpu.VMEM((ROUNDS, 2, n, tiles, LANES), F32),
-                pltpu.VMEM((n, 8, LANES), F32),
-                pltpu.VMEM((2, batch, k), F32),
+                pltpu.VMEM((2, k, batch), F32),
                 pltpu.VMEM((2, batch, width), F32),
                 pltpu.VMEM((k, width), F32),
                 sem((5,)),
-                sem((5,)),
-                sem((ROUNDS, 2, n - 1)),
-                sem((ROUNDS, 2, n - 1)),
-                sem((n - 1,)),
-                sem((n - 1,)),
-                sem((n - 1,)),
-                sem((n - 1,)),
             ],
-            compiler_params=pltpu.CompilerParams(collective_id=0, has_side_effects=True),
-        )(z_one, z_two, protos, queue_one, queue_two)
-        codes_one, codes_two, loss, dz_one, dz_two, grad_protos = outs
-        return codes_one, codes_two, loss[0, 0], dz_one, dz_two, grad_protos
+            compiler_params=pltpu.CompilerParams(vmem_limit_bytes=14 << 20),
+            name="grads",
+        )(*shared)
+        return codes_one.T, codes_two.T, loss[0, 0], dz_one, dz_two, grad_protos
 
     row_spec = P("data", None)
     full_spec = P(None, None)

time: 29.3 us -> 22.3 us (0.76)
  local copies, waits for them, and re-layouts: 5.33 us -> 0 us
  between operations: 2.41 us -> 0.64 us
    unnamed x13 -> x0, local copies, waits for them, and re-layouts: 5.33 us -> none
    pallas_call x1 -> x2, Pallas kernels: 21.4 us -> 21.5 us  [the longest x1 16.3 us: local_step(): pl.pallas_call(functools.partial(sums_kernel, n, k, batch, queue), out_sh...]
where the time goes in v2:
time: 22.3 us; the launch traced here: 22.2 us
  Pallas kernels  21.5 us (96%)
  between operations  0.64 us (3%)
    pallas_call x1, Pallas kernels, local_step(): pl.pallas_call(functools.partial(sums_kernel, n, k, batch, queue), out_sh...  16.3 us
    pallas_call x1, Pallas kernels, local_step(): pl.pallas_call(functools.partial(grads_kernel, n, k, batch), out_shape=(j...  5.27 us

profile of v2, /device:TPU:0, one launch (start us, length us, event | category | flops | bytes accessed | tf_op | source)
XLA Modules:
  0.0 22.2 jit_solution(1327151966959945199)
XLA Ops:
  0.6 16.3 %sums.1 = (f32[2,8,1024,128]{3,2,1,0:T(8,128)S(1)}, f32[2,8,1024,128]{3,2,1,0:T(8,128)S(1)}, f32[2,8,1024,128]{3,2,1,0:T(8,128)S(1)}, bf16[2,128,1024]{2,1,0:T(8...) custom-call(bf16[128,128]{1,0:T(8,128)(2,1)} %z1_hbm.1, ...), custom_call_target="tpu_custom_call" | custom-call | tf_op jit(solution)/shard_map/sums/pallas_call | solution.py:306
  16.9 5.3 %grads.1 = (f32[1000,128]{1,0:T(8,128)}, f32[1000,128]{1,0:T(8,128)}, f32[1,1]{1,0:T(1,128)}, f32[128,128]{1,0:T(8,128)}, f32[128,128]{1,0:T(8,128)}, /*index=5*/f32[1000,128]{1,0:T(8,128)}) custom-call(f32[2,8,1024,128]{3,2,1,0:T(8,128)S(1)} %get-tuple-element.19.aall, f32[2,8,1024,128]{3,2,1,0:T(8,128)S(1)} %get-tuple-element.20.pall, ...), custom_call_target="tpu_custom_call" | custom-call | tf_op jit(solution)/shard_map/grads/pallas_call | solution.py:336

commit v3 on v2

v3 whole, which is shorter than its diff:
```python
import functools
import math

import jax
import jax.numpy as jnp
from jax import lax
from jax.experimental import pallas as pl
from jax.experimental.pallas import tpu as pltpu
from jax.sharding import PartitionSpec as P

EPSILON = 0.05
TEMPERATURE = 0.1
ROUNDS = 3
LANES = 128
MESH = pl.DeviceIdType.MESH
F32 = jnp.float32
BF16 = jnp.bfloat16
NT = (((1,), (1,)), ((), ()))


def fold(x):
    return jnp.sum(x.reshape(x.shape[0] // 8, 8, LANES), axis=0)


def sums_kernel(
    n, protos, batch, queue,
    z1_hbm, z2_hbm, c_hbm, q1_hbm, q2_hbm,
    aall, pall, rinv, zt, cpad, wbuf, loss_part, lse_sum,
    xbuf, zall, sall, atr, cpart, csum,
    in_sem, send_sem, recv_sem, zsend_sem, zrecv_sem,
):
    tiles = cpad.shape[0] // LANES
    rows = batch + queue
    total_rows = n * rows
    coef = 1.0 / (2 * n * batch * TEMPERATURE)
    scale10 = math.log2(math.e) / TEMPERATURE

    me = lax.axis_index("data")
    bit0 = lax.rem(me, 2)
    bit1 = lax.rem(me // 2, 2)
    bit2 = me // 4

    def peer(k):
        b0, b1, b2 = k % 2, (k // 2) % 2, k // 4
        return (lax.rem(bit2 + b2, 2) * 2 + lax.rem(bit1 + b1, 2)) * 2 + lax.rem(bit0 + b0, 2)

    far_first = (6, 7, 4, 5, 2, 3, 1)

    c_in = pltpu.make_async_copy(c_hbm, cpad.at[pl.ds(0, protos)], in_sem.at[2])

    def rows_in(v):
        z_hbm, q_hbm = ((z1_hbm, q1_hbm), (z2_hbm, q2_hbm))[v]
        pltpu.make_async_copy(z_hbm, xbuf.at[v, pl.ds(0, batch)], in_sem.at[v]).start()
        pltpu.make_async_copy(q_hbm, xbuf.at[v, pl.ds(batch, queue)], in_sem.at[v]).start()

    def wait_rows(v):
        pltpu.make_async_copy(xbuf.at[v], xbuf.at[v], in_sem.at[v]).wait()

    c_in.start()
    rows_in(0)
    rows_in(1)

    barrier = pltpu.get_barrier_semaphore()
    for k in far_first:
        pl.semaphore_signal(barrier, inc=1, device_id=(peer(k),), device_id_type=MESH)

    cpad[pl.ds(protos, cpad.shape[0] - protos), :] = jnp.zeros((cpad.shape[0] - protos, LANES), BF16)
    c_in.wait()

    lane = lax.broadcasted_iota(jnp.int32, (1, LANES), 1)
    tail_ok = lane < (protos - (tiles - 1) * LANES)
    tail_mask = tail_ok.astype(F32)

    def publish(t, v, acc):
        for j in range(tiles):
            cpart[v, pl.ds(8 * j, 8), :] = acc[j]
        out = cpart[v, pl.ds(0, tiles, stride=8), :]
        for s in range(1, 8):
            out = out + cpart[v, pl.ds(s, tiles, stride=8), :]
        csum[t, v, me] = out

    def sum_copy(t, v, k, slots):
        return pltpu.make_async_remote_copy(
            src_ref=csum.at[t, v, slots], dst_ref=csum.at[t, v, slots],
            send_sem=send_sem.at[v], recv_sem=recv_sem.at[t, v],
            device_id=(peer(k),), device_id_type=MESH)

    def all_sums(t, v):
        return sum_copy(t, v, 1, pl.ds(0, n - 1))

    def send_sums(t, v):
        if t > 0:
            all_sums(t, v).wait_send()
        for k in far_first:
            sum_copy(t, v, k, me).start()

    def col_scale(t, v):
        all_sums(t, v).wait_recv()
        c = csum[t, v, 0]
        for d in range(1, n):
            c = c + csum[t, v, d]
        w = 1.0 / (protos * c)
        index = (lax.broadcasted_iota(jnp.int32, (tiles, LANES), 0) * LANES
                 + lax.broadcasted_iota(jnp.int32, (tiles, LANES), 1))
        wbuf[v] = jnp.where(index < protos, w, 0.0)

    def first_pass(v):
        acc = [jnp.zeros((8, LANES), F32) for _ in range(tiles)]
        for start, size in ((0, rows // 2), (rows // 2, rows // 2)):
            x = xbuf[v, pl.ds(start, size), :]
            for jj in range(tiles // 2):
                s = lax.dot_general(x, cpad[pl.ds(jj * 256, 256), :], NT, preferred_element_type=F32)
                for h in range(2):
                    e = jnp.exp2(s[:, h * LANES:(h + 1) * LANES] * scale10)
                    a = e * e
                    atr[v, 2 * jj + h, pl.ds(start, size), :] = a
                    acc[2 * jj + h] = acc[2 * jj + h] + fold(a)
        return acc

    def sink_pass(v):
        acc = [jnp.zeros((8, LANES), F32) for _ in range(tiles)]
        step = 128
        for b in range(rows // step):
            sl = pl.ds(b * step, step)
            p = atr[v, 0, sl, :] * wbuf[v, 0:1, :]
            for j in range(1, tiles):
                p = p + atr[v, j, sl, :] * wbuf[v, j:j + 1, :]
            u = 1.0 / (total_rows * jnp.sum(p, axis=1, keepdims=True))
            for j in range(tiles):
                acc[j] = acc[j] + fold(atr[v, j, sl, :] * u)
        return acc

    wait_rows(0)
    publish(0, 0, first_pass(0))
    pl.semaphore_wait(barrier, n - 1)
    send_sums(0, 0)
    wait_rows(1)
    publish(0, 1, first_pass(1))
    send_sums(0, 1)

    def z_copy(k, target, src, dst):
        return pltpu.make_async_remote_copy(
            src_ref=src, dst_ref=dst, send_sem=zsend_sem.at[0], recv_sem=zrecv_sem.at[k - 1],
            device_id=(peer(target),), device_id_type=MESH)

    for k in (6, 2, 4, 1):
        for v in range(2):
            z_copy(k, k, xbuf.at[v, pl.ds(0, batch)], zall.at[me, v]).start()

    def z_arrived(k):
        z_copy(k, k, zall.at[peer(k)], zall.at[peer(k)]).wait_recv()

    def relay(k):
        z_arrived(k)
        z_copy(k + 1, 1, zall.at[peer(k)], zall.at[peer(k)]).start()

    def prepare(k):
        d = peer(k)
        if k in (3, 5, 7, 1):
            z_arrived(k)
        sl = pl.ds(pl.multiple_of(d * batch, batch), batch)
        z = [xbuf[v, pl.ds(0, batch), :] if k == 0 else zall[d, v] for v in range(2)]
        for v in range(2):
            zt[:, pl.ds(pl.multiple_of((v * n + d) * batch, batch), batch)] = z[v].T
        x = jnp.concatenate(z, axis=0)
        p = None
        for jj in range(tiles // 2):
            s = lax.dot_general(x, cpad[pl.ds(jj * 256, 256), :], NT, preferred_element_type=F32)
            for h in range(2):
                j = 2 * jj + h
                sj = s[:, h * LANES:(h + 1) * LANES]
                e = jnp.exp2(sj * scale10)
                if j == tiles - 1:
                    e = e * tail_mask
                a = e * e
                for v in range(2):
                    half = slice(v * batch, (v + 1) * batch)
                    aall[v, j, sl, :] = a[half]
                    pall[v, j, sl, :] = e[half]
                    sall[v, j, sl, :] = sj[half]
                p = e if p is None else p + e
        r = jnp.sum(p, axis=1, keepdims=True)
        inv = coef / r
        lse_sum[d] = fold(jnp.broadcast_to(jnp.log(r), (2 * batch, LANES)))
        for v in range(2):
            for j in range(tiles):
                pall[v, j, sl, :] = pall[v, j, sl, :] * inv[v * batch:(v + 1) * batch]

    prepare(0)
    for v in range(2):
        col_scale(0, v)
        publish(1, v, sink_pass(v))
        send_sums(1, v)

    prepare(1)
    for k in (2, 4, 6):
        relay(k)
    for k in (2, 4):
        prepare(k)
    for v in range(2):
        col_scale(1, v)
        publish(2, v, sink_pass(v))
        send_sums(2, v)
    for k in (6, 3, 5, 7):
        prepare(k)


    def row_scale(v):
        part = jnp.zeros((8, LANES), F32)
        for d in range(n):
            sl = pl.ds(d * batch, batch)
            p = None
            m = None
            for j in range(tiles):
                t = aall[v, j, sl, :] * wbuf[v, j:j + 1, :]
                u = t * sall[1 - v, j, sl, :]
                p = t if p is None else p + t
                m = u if m is None else m + u
            inv = 1.0 / jnp.sum(p, axis=1, keepdims=True)
            part = part + fold(m * inv)
            rinv[v, sl, :] = jnp.broadcast_to(inv, (batch, LANES))
        return part

    col_scale(2, 0)
    part = row_scale(0)
    col_scale(2, 1)
    loss_part[...] = part + row_scale(1)

    for v in range(2):
        all_sums(2, v).wait_send()
    z_copy(1, 1, zall.at[pl.ds(0, n - 1)], zall.at[pl.ds(0, n - 1)]).wait_send()


def grads_kernel(
    n, protos, batch,
    aall, pall, rinv, zt, cpad, wbuf, loss_part, lse_sum,
    codes1_hbm, codes2_hbm, loss_ref, dz1_hbm, dz2_hbm, gp_hbm,
    gbuf, codes, dz, gp, out_sem,
):
    tiles = cpad.shape[0] // LANES
    batch_total = n * batch
    coef = 1.0 / (2 * batch_total * TEMPERATURE)
    me = lax.axis_index("data")
    own = pl.ds(pl.multiple_of(me * batch, batch), batch)
    codes_hbm = (codes1_hbm, codes2_hbm)
    dz_hbm = (dz1_hbm, dz2_hbm)

    for jj in range(tiles // 2):
        size = min(2 * LANES, protos - jj * 2 * LANES)
        cols = pl.ds(jj * 2 * LANES, size)
        for v in range(2):
            for h in range(2):
                j = 2 * jj + h
                w = wbuf[v, j:j + 1, :] * coef
                for d in range(n):
                    sl = pl.ds(d * batch, batch)
                    g = pall[1 - v, j, sl, :] - aall[v, j, sl, :] * w * rinv[v, sl, :]
                    gbuf[jj, pl.ds(((1 - v) * n + d) * batch, batch), h * LANES:(h + 1) * LANES] = g.astype(BF16)
                part = min(LANES, protos - j * LANES)
                q = aall[v, j, own, :] * wbuf[v, j:j + 1, :] * rinv[v, own, :]
                codes[v, pl.ds(j * LANES, part), :] = q.T[:part]
            pltpu.make_async_copy(codes.at[v, cols], codes_hbm[v].at[cols], out_sem.at[v]).start()
        g = jnp.dot(zt[...], gbuf[jj], preferred_element_type=F32)
        gp[cols, :] = g.T[:size]
        pltpu.make_async_copy(gp.at[cols], gp_hbm.at[cols], out_sem.at[4]).start()
        for v in range(2):
            rows = pl.ds(pl.multiple_of((v * n + me) * batch, batch), batch)
            o = jnp.dot(gbuf[jj, rows, :], cpad[pl.ds(jj * 2 * LANES, 2 * LANES), :], preferred_element_type=F32)
            dz[v] = o if jj == 0 else dz[v] + o
    for v in range(2):
        pltpu.make_async_copy(dz.at[v], dz_hbm[v], out_sem.at[2 + v]).start()

    logs = lse_sum[0]
    for d in range(1, n):
        logs = logs + lse_sum[d]
    total = jnp.sum(loss_part[...]) * (1.0 / TEMPERATURE) - jnp.sum(logs) * (1.0 / LANES)
    loss_ref[0, 0] = total * (-1.0 / (2 * batch_total))

    for v in range(2):
        pltpu.make_async_copy(codes.at[v], codes_hbm[v], out_sem.at[v]).wait()
        pltpu.make_async_copy(dz.at[v], dz_hbm[v], out_sem.at[2 + v]).wait()
    pltpu.make_async_copy(gp, gp_hbm, out_sem.at[4]).wait()


def solution(mesh):
    n = mesh.shape["data"]

    def local_step(z_one, z_two, protos, queue_one, queue_two):
        k, width = protos.shape
        batch, queue = z_one.shape[0], queue_one.shape[0]
        rows = batch + queue
        pad = (k + 255) // 256 * 256
        tiles = pad // LANES
        anywhere = pl.BlockSpec(memory_space=pl.ANY)
        sem = pltpu.SemaphoreType.DMA
        vmem = pl.BlockSpec(memory_space=pltpu.VMEM)
        whole = n * batch
        shared = pl.pallas_call(
            functools.partial(sums_kernel, n, k, batch, queue),
            out_shape=(
                pltpu.VMEM((2, tiles, whole, LANES), F32),
                pltpu.VMEM((2, tiles, whole, LANES), F32),
                pltpu.VMEM((2, whole, LANES), F32),
                pltpu.VMEM((width, 2 * whole), BF16),
                pltpu.VMEM((pad, width), BF16),
                pltpu.VMEM((2, tiles, LANES), F32),
                pltpu.VMEM((8, LANES), F32),
                pltpu.VMEM((n, 8, LANES), F32),
            ),
            in_specs=[anywhere] * 5,
            out_specs=(vmem,) * 8,
            scratch_shapes=[
                pltpu.VMEM((2, rows, width), BF16),
                pltpu.VMEM((n, 2, batch, width), BF16),
                pltpu.VMEM((2, tiles, whole, LANES), F32),
                pltpu.VMEM((2, tiles, rows, LANES), F32),
                pltpu.VMEM((2, 8 * tiles, LANES), F32),
                pltpu.VMEM((ROUNDS, 2, n, tiles, LANES), F32),
                sem((3,)),
                sem((2,)),
                sem((ROUNDS, 2)),
                sem((1,)),
                sem((n - 1,)),
            ],
            compiler_params=pltpu.CompilerParams(
                collective_id=0, has_side_effects=True, vmem_limit_bytes=20 << 20),
            name="sums",
        )(*(pltpu.with_memory_space_constraint(x, pltpu.HBM) for x in (z_one, z_two, protos, queue_one, queue_two)))
        codes_one, codes_two, loss, dz_one, dz_two, grad_protos = pl.pallas_call(
            functools.partial(grads_kernel, n, k, batch),
            out_shape=(
                jax.ShapeDtypeStruct((k, batch), F32),
                jax.ShapeDtypeStruct((k, batch), F32),
                jax.ShapeDtypeStruct((1, 1), F32),
                jax.ShapeDtypeStruct((batch, width), F32),
                jax.ShapeDtypeStruct((batch, width), F32),
                jax.ShapeDtypeStruct((k, width), F32),
            ),
            in_specs=[vmem] * 8,
            out_specs=(anywhere, anywhere, pl.BlockSpec(memory_space=pltpu.SMEM), anywhere, anywhere, anywhere),
            scratch_shapes=[
                pltpu.VMEM((tiles // 2, 2 * whole, 2 * LANES), BF16),
                pltpu.VMEM((2, k, batch), F32),
                pltpu.VMEM((2, batch, width), F32),
                pltpu.VMEM((k, width), F32),
                sem((5,)),
            ],
            compiler_params=pltpu.CompilerParams(vmem_limit_bytes=14 << 20),
            name="grads",
        )(*shared)
        return codes_one.T, codes_two.T, loss[0, 0], dz_one, dz_two, grad_protos

    row_spec = P("data", None)
    full_spec = P(None, None)
    return jax.shard_map(
        local_step,
        mesh=mesh,
        in_specs=(row_spec, row_spec, full_spec, row_spec, row_spec),
        out_specs=(row_spec, row_spec, P(), row_spec, row_spec, full_spec),
        check_vma=False,
    )
```

time: 22.3 us -> 20.8 us (0.933)
  Pallas kernels: 21.5 us -> 20 us
    pallas_call x1, Pallas kernels: 5.27 us -> 3.75 us  [local_step(): pl.pallas_call(functools.partial(grads_kernel, n, k, batch), out_shape=(j...]
where the time goes in v3:
time: 20.8 us; the launch traced here: 20.6 us
  Pallas kernels  20 us (96%)
  between operations  0.64 us (3%)
    pallas_call x1, Pallas kernels, local_step(): pl.pallas_call(functools.partial(sums_kernel, n, k, batch, queue), out_sh...  16.2 us
    pallas_call x1, Pallas kernels, local_step(): pl.pallas_call(functools.partial(grads_kernel, n, k, batch), out_shape=(j...  3.75 us

profile of v3, /device:TPU:0, one launch (start us, length us, event | category | flops | bytes accessed | tf_op | source)
XLA Modules:
  0.0 20.6 jit_solution(532909741635909365)
XLA Ops:
  0.6 16.2 %sums.1 = (f32[2,8,1024,128]{3,2,1,0:T(8,128)S(1)}, f32[2,8,1024,128]{3,2,1,0:T(8,128)S(1)}, f32[2,1024,128]{2,1,0:T(8,128)S(1)}, bf16[128,2048]{1,0:T(8,128)(2,...) custom-call(bf16[128,128]{1,0:T(8,128)(2,1)} %z1_hbm.1, ...), custom_call_target="tpu_custom_call" | custom-call | tf_op jit(solution)/shard_map/sums/pallas_call | solution.py:298
  16.9 3.7 %grads.1 = (f32[1000,128]{1,0:T(8,128)}, f32[1000,128]{1,0:T(8,128)}, f32[1,1]{1,0:T(1,128)}, f32[128,128]{1,0:T(8,128)}, f32[128,128]{1,0:T(8,128)}, /*index=5*/f32[1000,128]{1,0:T(8,128)}) custom-call(f32[2,8,1024,128]{3,2,1,0:T(8,128)S(1)} %get-tuple-element.20.aall, f32[2,8,1024,128]{3,2,1,0:T(8,128)S(1)} %get-tuple-element.21.pall, ...), custom_call_target="tpu_custom_call" | custom-call | tf_op jit(solution)/shard_map/grads/pallas_call | solution.py:329

commit v4 on v3

--- a/solution.py
+++ b/solution.py
@@ -25,7 +25,7 @@
 def sums_kernel(
     n, protos, batch, queue,
     z1_hbm, z2_hbm, c_hbm, q1_hbm, q2_hbm,
-    aall, pall, rinv, zt, cpad, wbuf, loss_part, lse_sum,
+    aall, pall, rinv, zt, cpad, small, lse_sum,
     xbuf, zall, sall, atr, cpart, csum,
     in_sem, send_sem, recv_sem, zsend_sem, zrecv_sem,
 ):
@@ -102,7 +102,7 @@
         w = 1.0 / (protos * c)
         index = (lax.broadcasted_iota(jnp.int32, (tiles, LANES), 0) * LANES
                  + lax.broadcasted_iota(jnp.int32, (tiles, LANES), 1))
-        wbuf[v] = jnp.where(index < protos, w, 0.0)
+        small[v] = jnp.where(index < protos, w, 0.0)
 
     def first_pass(v):
         acc = [jnp.zeros((8, LANES), F32) for _ in range(tiles)]
@@ -122,9 +122,9 @@
         step = 128
         for b in range(rows // step):
             sl = pl.ds(b * step, step)
-            p = atr[v, 0, sl, :] * wbuf[v, 0:1, :]
+            p = atr[v, 0, sl, :] * small[v, 0:1, :]
             for j in range(1, tiles):
-                p = p + atr[v, j, sl, :] * wbuf[v, j:j + 1, :]
+                p = p + atr[v, j, sl, :] * small[v, j:j + 1, :]
             u = 1.0 / (total_rows * jnp.sum(p, axis=1, keepdims=True))
             for j in range(tiles):
                 acc[j] = acc[j] + fold(atr[v, j, sl, :] * u)
@@ -206,25 +206,37 @@
 
 
     def row_scale(v):
-        part = jnp.zeros((8, LANES), F32)
-        for d in range(n):
+        w = [small[v, j:j + 1, :] for j in range(tiles)]
+
+        def sums(d):
             sl = pl.ds(d * batch, batch)
             p = None
             m = None
             for j in range(tiles):
-                t = aall[v, j, sl, :] * wbuf[v, j:j + 1, :]
+                t = aall[v, j, sl, :] * w[j]
                 u = t * sall[1 - v, j, sl, :]
                 p = t if p is None else p + t
                 m = u if m is None else m + u
-            inv = 1.0 / jnp.sum(p, axis=1, keepdims=True)
-            part = part + fold(m * inv)
-            rinv[v, sl, :] = jnp.broadcast_to(inv, (batch, LANES))
-        return part
+            return jnp.sum(p, axis=1, keepdims=True), m
+
+        def scale(d, p, m):
+            inv = 1.0 / p
+            rinv[v, pl.ds(d * batch, batch), :] = jnp.broadcast_to(inv, (batch, LANES))
+            return fold(m * inv)
+
+        part = jnp.zeros((8, LANES), F32)
+        last = None
+        for d in range(n):
+            this = sums(d)
+            if d > 0:
+                part = part + scale(d - 1, *last)
+            last = this
+        return part + scale(n - 1, *last)
 
     col_scale(2, 0)
     part = row_scale(0)
     col_scale(2, 1)
-    loss_part[...] = part + row_scale(1)
+    small[2] = part + row_scale(1)
 
     for v in range(2):
         all_sums(2, v).wait_send()
@@ -233,9 +245,9 @@
 
 def grads_kernel(
     n, protos, batch,
-    aall, pall, rinv, zt, cpad, wbuf, loss_part, lse_sum,
+    aall, pall, rinv, zt, cpad, small, lse_sum,
     codes1_hbm, codes2_hbm, loss_ref, dz1_hbm, dz2_hbm, gp_hbm,
-    gbuf, codes, dz, gp, out_sem,
+    gbuf, codes, gp, dz, out_sem,
 ):
     tiles = cpad.shape[0] // LANES
     batch_total = n * batch
@@ -245,41 +257,84 @@
     codes_hbm = (codes1_hbm, codes2_hbm)
     dz_hbm = (dz1_hbm, dz2_hbm)
 
-    for jj in range(tiles // 2):
-        size = min(2 * LANES, protos - jj * 2 * LANES)
-        cols = pl.ds(jj * 2 * LANES, size)
+    pairs = tiles // 2
+    deep = 2 * batch
+
+    def cols_of(jj):
+        return pl.ds(jj * 2 * LANES, min(2 * LANES, protos - jj * 2 * LANES))
+
+    def body(acc, dz_acc):
+        for ref in (*acc[0], *acc[1], dz_acc):
+            pltpu.matmul_pop(ref)
+
+        def tile(jj, v):
+            w = [small[v, 2 * jj + h:2 * jj + h + 1, :] * coef for h in range(2)]
+            for d in range(0, n, 2):
+                halves = []
+                for h in range(2):
+                    sl = pl.ds(d * batch, deep)
+                    j = 2 * jj + h
+                    g = pall[1 - v, j, sl, :] - aall[v, j, sl, :] * w[h] * rinv[v, sl, :]
+                    halves.append(g.astype(BF16))
+                g = jnp.concatenate(halves, axis=1)
+                gbuf[jj % 2, pl.ds((1 - v) * n * batch + d * batch, deep), :] = g
+                unit = (d // 2) % 2
+                pltpu.matmul_push_rhs(g, staging_register=0, mxu_index=unit)
+                pltpu.matmul_acc_lhs(
+                    acc[jj % 2][unit], zt[:, pl.ds((1 - v) * n * batch + d * batch, deep)], load_staged_rhs=0)
+
+        def own_part(jj):
+            for v in range(2):
+                for h in range(2):
+                    j = 2 * jj + h
+                    part = min(LANES, protos - j * LANES)
+                    q = aall[v, j, own, :] * small[v, j:j + 1, :] * rinv[v, own, :]
+                    codes[v, pl.ds(j * LANES, part), :] = q.T[:part]
+            c = cpad[pl.ds(jj * 2 * LANES, 2 * LANES), :]
+            pltpu.matmul_push_rhs(jnp.concatenate([c, c], axis=1), staging_register=1, mxu_index=0)
+            g = jnp.concatenate(
+                [gbuf[jj % 2, pl.ds(pl.multiple_of((v * n + me) * batch, batch), batch), :] for v in range(2)], axis=0)
+            pltpu.matmul_acc_lhs(dz_acc, g, load_staged_rhs=1)
+
+        def drain(jj):
+            g = pltpu.matmul_pop(acc[jj % 2][0]) + pltpu.matmul_pop(acc[jj % 2][1])
+            cols = cols_of(jj)
+            gp[cols, :] = g.T[:cols.size]
+
+        def send(jj):
+            cols = cols_of(jj)
+            pltpu.make_async_copy(gp.at[cols], gp_hbm.at[cols], out_sem.at[4]).start()
+            for v in range(2):
+                pltpu.make_async_copy(codes.at[v, cols], codes_hbm[v].at[cols], out_sem.at[v]).start()
+
+        for jj in range(pairs):
+            tile(jj, 0)
+            if jj > 0:
+                drain(jj - 1)
+            tile(jj, 1)
+            own_part(jj)
+            if jj > 0:
+                send(jj - 1)
+        drain(pairs - 1)
+        send(pairs - 1)
+        o = pltpu.matmul_pop(dz_acc)
         for v in range(2):
-            for h in range(2):
-                j = 2 * jj + h
-                w = wbuf[v, j:j + 1, :] * coef
-                for d in range(n):
-                    sl = pl.ds(d * batch, batch)
-                    g = pall[1 - v, j, sl, :] - aall[v, j, sl, :] * w * rinv[v, sl, :]
-                    gbuf[jj, pl.ds(((1 - v) * n + d) * batch, batch), h * LANES:(h + 1) * LANES] = g.astype(BF16)
-                part = min(LANES, protos - j * LANES)
-                q = aall[v, j, own, :] * wbuf[v, j:j + 1, :] * rinv[v, own, :]
-                codes[v, pl.ds(j * LANES, part), :] = q.T[:part]
-            pltpu.make_async_copy(codes.at[v, cols], codes_hbm[v].at[cols], out_sem.at[v]).start()
-        g = jnp.dot(zt[...], gbuf[jj], preferred_element_type=F32)
-        gp[cols, :] = g.T[:size]
-        pltpu.make_async_copy(gp.at[cols], gp_hbm.at[cols], out_sem.at[4]).start()
-        for v in range(2):
-            rows = pl.ds(pl.multiple_of((v * n + me) * batch, batch), batch)
-            o = jnp.dot(gbuf[jj, rows, :], cpad[pl.ds(jj * 2 * LANES, 2 * LANES), :], preferred_element_type=F32)
-            dz[v] = o if jj == 0 else dz[v] + o
-    for v in range(2):
-        pltpu.make_async_copy(dz.at[v], dz_hbm[v], out_sem.at[2 + v]).start()
+            dz[v] = o[v * batch:(v + 1) * batch, :LANES]
+            pltpu.make_async_copy(dz.at[v], dz_hbm[v], out_sem.at[2 + v]).start()
+
+    half = lambda unit: pltpu.ACC(unit)((LANES, 2 * LANES), F32)
+    pl.run_scoped(body, ((half(0), half(1)), (half(0), half(1))), pltpu.ACC(0)((deep, 2 * LANES), F32))
 
     logs = lse_sum[0]
     for d in range(1, n):
         logs = logs + lse_sum[d]
-    total = jnp.sum(loss_part[...]) * (1.0 / TEMPERATURE) - jnp.sum(logs) * (1.0 / LANES)
+    total = jnp.sum(small[2]) * (1.0 / TEMPERATURE) - jnp.sum(logs) * (1.0 / LANES)
     loss_ref[0, 0] = total * (-1.0 / (2 * batch_total))
 
     for v in range(2):
-        pltpu.make_async_copy(codes.at[v], codes_hbm[v], out_sem.at[v]).wait()
+        pltpu.make_async_copy(codes.at[v, pl.ds(0, protos)], codes_hbm[v], out_sem.at[v]).wait()
         pltpu.make_async_copy(dz.at[v], dz_hbm[v], out_sem.at[2 + v]).wait()
-    pltpu.make_async_copy(gp, gp_hbm, out_sem.at[4]).wait()
+    pltpu.make_async_copy(gp.at[pl.ds(0, protos)], gp_hbm, out_sem.at[4]).wait()
 
 
 def solution(mesh):
@@ -303,12 +358,11 @@
                 pltpu.VMEM((2, whole, LANES), F32),
                 pltpu.VMEM((width, 2 * whole), BF16),
                 pltpu.VMEM((pad, width), BF16),
-                pltpu.VMEM((2, tiles, LANES), F32),
-                pltpu.VMEM((8, LANES), F32),
+                pltpu.VMEM((4, tiles, LANES), F32),
                 pltpu.VMEM((n, 8, LANES), F32),
             ),
             in_specs=[anywhere] * 5,
-            out_specs=(vmem,) * 8,
+            out_specs=(vmem,) * 7,
             scratch_shapes=[
                 pltpu.VMEM((2, rows, width), BF16),
                 pltpu.VMEM((n, 2, batch, width), BF16),
@@ -336,13 +390,13 @@
                 jax.ShapeDtypeStruct((batch, width), F32),
                 jax.ShapeDtypeStruct((k, width), F32),
             ),
-            in_specs=[vmem] * 8,
+            in_specs=[vmem] * 7,
             out_specs=(anywhere, anywhere, pl.BlockSpec(memory_space=pltpu.SMEM), anywhere, anywhere, anywhere),
             scratch_shapes=[
-                pltpu.VMEM((tiles // 2, 2 * whole, 2 * LANES), BF16),
-                pltpu.VMEM((2, k, batch), F32),
+                pltpu.VMEM((2, 2 * whole, 2 * LANES), BF16),
+                pltpu.VMEM((2, pad, batch), F32),
+                pltpu.VMEM((pad, width), F32),
                 pltpu.VMEM((2, batch, width), F32),
-                pltpu.VMEM((k, width), F32),
                 sem((5,)),
             ],
             compiler_params=pltpu.CompilerParams(vmem_limit_bytes=14 << 20),

time: 20.8 us -> 19.8 us (0.952)
  Pallas kernels: 20 us -> 19.1 us
    pallas_call x1, Pallas kernels: 3.75 us -> 3.1 us  [local_step(): pl.pallas_call(functools.partial(grads_kernel, n, k, batch), out_shape=(j...]
    pallas_call x1, Pallas kernels: 16.2 us -> 16 us  [local_step(): pl.pallas_call(functools.partial(sums_kernel, n, k, batch, queue), out_sh...]
where the time goes in v4:
time: 19.8 us; the launch traced here: 19.7 us
  Pallas kernels  19.1 us (96%)
  between operations  0.64 us (3%)
    pallas_call x1, Pallas kernels, local_step(): pl.pallas_call(functools.partial(sums_kernel, n, k, batch, queue), out_sh...  16 us
    pallas_call x1, Pallas kernels, local_step(): pl.pallas_call(functools.partial(grads_kernel, n, k, batch), out_shape=(j...  3.1 us

profile of v4, /device:TPU:0, one launch (start us, length us, event | category | flops | bytes accessed | tf_op | source)
XLA Modules:
  0.0 19.7 jit_solution(4631398224548018123)
XLA Ops:
  0.6 16.0 %sums.1 = (f32[2,8,1024,128]{3,2,1,0:T(8,128)S(1)}, f32[2,8,1024,128]{3,2,1,0:T(8,128)S(1)}, f32[2,1024,128]{2,1,0:T(8,128)S(1)}, bf16[128,2048]{1,0:T(8,128)(2,...) custom-call(bf16[128,128]{1,0:T(8,128)(2,1)} %z1_hbm.1, ...), custom_call_target="tpu_custom_call" | custom-call | tf_op jit(solution)/shard_map/sums/pallas_call | solution.py:353
  16.6 3.1 %grads.1 = (f32[1000,128]{1,0:T(8,128)}, f32[1000,128]{1,0:T(8,128)}, f32[1,1]{1,0:T(1,128)}, f32[128,128]{1,0:T(8,128)}, f32[128,128]{1,0:T(8,128)}, /*index=5*/f32[1000,128]{1,0:T(8,128)}) custom-call(f32[2,8,1024,128]{3,2,1,0:T(8,128)S(1)} %get-tuple-element.19.aall, f32[2,8,1024,128]{3,2,1,0:T(8,128)S(1)} %get-tuple-element.20.pall, ...), custom_call_target="tpu_custom_call" | custom-call | tf_op jit(solution)/shard_map/grads/pallas_call | solution.py:383

commit v5 on v4

--- a/solution.py
+++ b/solution.py
@@ -161,7 +161,7 @@
         sl = pl.ds(pl.multiple_of(d * batch, batch), batch)
         z = [xbuf[v, pl.ds(0, batch), :] if k == 0 else zall[d, v] for v in range(2)]
         for v in range(2):
-            zt[:, pl.ds(pl.multiple_of((v * n + d) * batch, batch), batch)] = z[v].T
+            zt[:, pl.ds(pl.multiple_of((v * n + d) * batch, batch), batch)] = z[v].astype(F32).T
         x = jnp.concatenate(z, axis=0)
         p = None
         for jj in range(tiles // 2):
@@ -214,6 +214,7 @@
             m = None
             for j in range(tiles):
                 t = aall[v, j, sl, :] * w[j]
+                aall[v, j, sl, :] = t
                 u = t * sall[1 - v, j, sl, :]
                 p = t if p is None else p + t
                 m = u if m is None else m + u
@@ -221,7 +222,7 @@
 
         def scale(d, p, m):
             inv = 1.0 / p
-            rinv[v, pl.ds(d * batch, batch), :] = jnp.broadcast_to(inv, (batch, LANES))
+            rinv[v, pl.ds(d * batch, batch), :] = jnp.broadcast_to(coef * inv, (batch, LANES))
             return fold(m * inv)
 
         part = jnp.zeros((8, LANES), F32)
@@ -246,8 +247,8 @@
 def grads_kernel(
     n, protos, batch,
     aall, pall, rinv, zt, cpad, small, lse_sum,
-    codes1_hbm, codes2_hbm, loss_ref, dz1_hbm, dz2_hbm, gp_hbm,
-    gbuf, codes, gp, dz, out_sem,
+    codes1_hbm, codes2_hbm, loss_hbm, dz1_hbm, dz2_hbm, gp_hbm,
+    codes, gp, dz, loss, out_sem,
 ):
     tiles = cpad.shape[0] // LANES
     batch_total = n * batch
@@ -257,84 +258,95 @@
     codes_hbm = (codes1_hbm, codes2_hbm)
     dz_hbm = (dz1_hbm, dz2_hbm)
 
-    pairs = tiles // 2
-    deep = 2 * batch
-
-    def cols_of(jj):
-        return pl.ds(jj * 2 * LANES, min(2 * LANES, protos - jj * 2 * LANES))
-
-    def body(acc, dz_acc):
-        for ref in (*acc[0], *acc[1], dz_acc):
-            pltpu.matmul_pop(ref)
-
-        def tile(jj, v):
-            w = [small[v, 2 * jj + h:2 * jj + h + 1, :] * coef for h in range(2)]
-            for d in range(0, n, 2):
-                halves = []
-                for h in range(2):
-                    sl = pl.ds(d * batch, deep)
-                    j = 2 * jj + h
-                    g = pall[1 - v, j, sl, :] - aall[v, j, sl, :] * w[h] * rinv[v, sl, :]
-                    halves.append(g.astype(BF16))
-                g = jnp.concatenate(halves, axis=1)
-                gbuf[jj % 2, pl.ds((1 - v) * n * batch + d * batch, deep), :] = g
-                unit = (d // 2) % 2
-                pltpu.matmul_push_rhs(g, staging_register=0, mxu_index=unit)
-                pltpu.matmul_acc_lhs(
-                    acc[jj % 2][unit], zt[:, pl.ds((1 - v) * n * batch + d * batch, deep)], load_staged_rhs=0)
-
-        def own_part(jj):
-            for v in range(2):
-                for h in range(2):
-                    j = 2 * jj + h
-                    part = min(LANES, protos - j * LANES)
-                    q = aall[v, j, own, :] * small[v, j:j + 1, :] * rinv[v, own, :]
-                    codes[v, pl.ds(j * LANES, part), :] = q.T[:part]
-            c = cpad[pl.ds(jj * 2 * LANES, 2 * LANES), :]
-            pltpu.matmul_push_rhs(jnp.concatenate([c, c], axis=1), staging_register=1, mxu_index=0)
-            g = jnp.concatenate(
-                [gbuf[jj % 2, pl.ds(pl.multiple_of((v * n + me) * batch, batch), batch), :] for v in range(2)], axis=0)
-            pltpu.matmul_acc_lhs(dz_acc, g, load_staged_rhs=1)
-
-        def drain(jj):
-            g = pltpu.matmul_pop(acc[jj % 2][0]) + pltpu.matmul_pop(acc[jj % 2][1])
-            cols = cols_of(jj)
-            gp[cols, :] = g.T[:cols.size]
-
-        def send(jj):
-            cols = cols_of(jj)
-            pltpu.make_async_copy(gp.at[cols], gp_hbm.at[cols], out_sem.at[4]).start()
-            for v in range(2):
-                pltpu.make_async_copy(codes.at[v, cols], codes_hbm[v].at[cols], out_sem.at[v]).start()
-
-        for jj in range(pairs):
-            tile(jj, 0)
-            if jj > 0:
-                drain(jj - 1)
-            tile(jj, 1)
-            own_part(jj)
-            if jj > 0:
-                send(jj - 1)
-        drain(pairs - 1)
-        send(pairs - 1)
-        o = pltpu.matmul_pop(dz_acc)
-        for v in range(2):
-            dz[v] = o[v * batch:(v + 1) * batch, :LANES]
-            pltpu.make_async_copy(dz.at[v], dz_hbm[v], out_sem.at[2 + v]).start()
-
-    half = lambda unit: pltpu.ACC(unit)((LANES, 2 * LANES), F32)
-    pl.run_scoped(body, ((half(0), half(1)), (half(0), half(1))), pltpu.ACC(0)((deep, 2 * LANES), F32))
-
     logs = lse_sum[0]
     for d in range(1, n):
         logs = logs + lse_sum[d]
     total = jnp.sum(small[2]) * (1.0 / TEMPERATURE) - jnp.sum(logs) * (1.0 / LANES)
-    loss_ref[0, 0] = total * (-1.0 / (2 * batch_total))
+    loss[0, 0] = total * (-1.0 / (2 * batch_total))
+    pltpu.make_async_copy(loss, loss_hbm, out_sem.at[5]).start()
+
+    pairs = tiles // 2
+    deep = 2 * batch
+
+    def cols_of(jj):
+        return pl.ds(jj * 2 * LANES, min(2 * LANES, protos - jj * 2 * LANES))
+
+    def body(acc, dz_acc):
+        for ref in (*acc[0], *acc[1], *dz_acc):
+            pltpu.matmul_pop(ref)
+
+        def tiles_of(big, v):
+            for d in range(0, n, 2):
+                sl = pl.ds(d * batch, deep)
+                scale = rinv[v, sl, :]
+                lhs = zt[:, pl.ds((1 - v) * n * batch + d * batch, deep)]
+                reg = (d // 2) % 2
+                for unit in range(2):
+                    g = [pall[1 - v, j, sl, :] - aall[v, j, sl, :] * scale
+                         for j in (4 * big + 2 * unit, 4 * big + 2 * unit + 1)]
+                    pltpu.matmul_push_rhs(jnp.concatenate(g, axis=1), staging_register=reg, mxu_index=unit)
+                    pltpu.matmul_acc_lhs(acc[big][unit], lhs, load_staged_rhs=reg)
+
+        def own_part(jj):
+            lhs = []
+            for v in range(2):
+                g = []
+                for h in range(2):
+                    j = 2 * jj + h
+                    part = min(LANES, protos - j * LANES)
+                    q = aall[v, j, own, :] * rinv[v, own, :]
+                    g.append(pall[1 - v, j, own, :] - q)
+                    codes[v, pl.ds(j * LANES, part), :] = (q * (1.0 / coef)).T[:part]
+                lhs.insert(0, jnp.concatenate(g, axis=1))
+            c = cpad[pl.ds(jj * 2 * LANES, 2 * LANES), :].astype(F32)
+            pltpu.matmul_push_rhs(jnp.concatenate([c, c], axis=1), staging_register=0, mxu_index=jj % 2)
+            pltpu.matmul_acc_lhs(dz_acc[jj % 2], jnp.concatenate(lhs, axis=0), load_staged_rhs=0)
+
+        def drain(big):
+            for unit in range(2):
+                cols = cols_of(2 * big + unit)
+                gp[cols, :] = pltpu.matmul_pop(acc[big][unit]).T[:cols.size]
+
+        def send(big):
+            for jj in (2 * big, 2 * big + 1):
+                cols = cols_of(jj)
+                pltpu.make_async_copy(gp.at[cols], gp_hbm.at[cols], out_sem.at[4]).start()
+
+        def send_codes(big):
+            for jj in (2 * big, 2 * big + 1):
+                cols = cols_of(jj)
+                for v in range(2):
+                    pltpu.make_async_copy(codes.at[v, cols], codes_hbm[v].at[cols], out_sem.at[v]).start()
+
+        own_part(0)
+        own_part(1)
+        send_codes(0)
+        tiles_of(0, 0)
+        tiles_of(0, 1)
+        own_part(2)
+        own_part(3)
+        send_codes(1)
+        tiles_of(1, 0)
+        drain(0)
+        send(0)
+        o = pltpu.matmul_pop(dz_acc[0]) + pltpu.matmul_pop(dz_acc[1])
+        for v in range(2):
+            dz[v] = o[v * batch:(v + 1) * batch, :LANES]
+            pltpu.make_async_copy(dz.at[v], dz_hbm[v], out_sem.at[2 + v]).start()
+        tiles_of(1, 1)
+        drain(1)
+        send(1)
+
+    def acc_of(rows):
+        return tuple(pltpu.ACC(unit)((rows, 2 * LANES), F32) for unit in range(2))
+
+    pl.run_scoped(body, (acc_of(LANES), acc_of(LANES)), acc_of(deep))
 
     for v in range(2):
         pltpu.make_async_copy(codes.at[v, pl.ds(0, protos)], codes_hbm[v], out_sem.at[v]).wait()
         pltpu.make_async_copy(dz.at[v], dz_hbm[v], out_sem.at[2 + v]).wait()
     pltpu.make_async_copy(gp.at[pl.ds(0, protos)], gp_hbm, out_sem.at[4]).wait()
+    pltpu.make_async_copy(loss, loss_hbm, out_sem.at[5]).wait()
 
 
 def solution(mesh):
@@ -356,7 +368,7 @@
                 pltpu.VMEM((2, tiles, whole, LANES), F32),
                 pltpu.VMEM((2, tiles, whole, LANES), F32),
                 pltpu.VMEM((2, whole, LANES), F32),
-                pltpu.VMEM((width, 2 * whole), BF16),
+                pltpu.VMEM((width, 2 * whole), F32),
                 pltpu.VMEM((pad, width), BF16),
                 pltpu.VMEM((4, tiles, LANES), F32),
                 pltpu.VMEM((n, 8, LANES), F32),
@@ -391,13 +403,13 @@
                 jax.ShapeDtypeStruct((k, width), F32),
             ),
             in_specs=[vmem] * 7,
-            out_specs=(anywhere, anywhere, pl.BlockSpec(memory_space=pltpu.SMEM), anywhere, anywhere, anywhere),
+            out_specs=(anywhere,) * 6,
             scratch_shapes=[
-                pltpu.VMEM((2, 2 * whole, 2 * LANES), BF16),
                 pltpu.VMEM((2, pad, batch), F32),
                 pltpu.VMEM((pad, width), F32),
                 pltpu.VMEM((2, batch, width), F32),
-                sem((5,)),
+                pltpu.SMEM((1, 1), F32),
+                sem((6,)),
             ],
             compiler_params=pltpu.CompilerParams(vmem_limit_bytes=14 << 20),
             name="grads",

time: 19.8 us -> 19.1 us (0.965)
  Pallas kernels: 19.1 us -> 18.4 us
    pallas_call x1, Pallas kernels: 3.1 us -> 2.25 us  [local_step(): pl.pallas_call(functools.partial(grads_kernel, n, k, batch), out_shape=(j...]
where the time goes in v5:
time: 19.1 us; the launch traced here: 19 us
  Pallas kernels  18.4 us (96%)
  between operations  0.64 us (3%)
    pallas_call x1, Pallas kernels, local_step(): pl.pallas_call(functools.partial(sums_kernel, n, k, batch, queue), out_sh...  16.1 us
    pallas_call x1, Pallas kernels, local_step(): pl.pallas_call(functools.partial(grads_kernel, n, k, batch), out_shape=(j...  2.25 us

profile of v5, /device:TPU:0, one launch (start us, length us, event | category | flops | bytes accessed | tf_op | source)
XLA Modules:
  0.0 19.0 jit_solution(12118774710098586349)
XLA Ops:
  0.6 16.1 %sums.1 = (f32[2,8,1024,128]{3,2,1,0:T(8,128)S(1)}, f32[2,8,1024,128]{3,2,1,0:T(8,128)S(1)}, f32[2,1024,128]{2,1,0:T(8,128)S(1)}, f32[128,2048]{1,0:T(8,128)S(1)...) custom-call(bf16[128,128]{1,0:T(8,128)(2,1)} %z1_hbm.1, ...), custom_call_target="tpu_custom_call" | custom-call | tf_op jit(solution)/shard_map/sums/pallas_call | solution.py:365
  16.7 2.3 %grads.1 = (f32[1000,128]{1,0:T(8,128)}, f32[1000,128]{1,0:T(8,128)}, f32[1,1]{1,0:T(1,128)}, f32[128,128]{1,0:T(8,128)}, f32[128,128]{1,0:T(8,128)}, /*index=5*/f32[1000,128]{1,0:T(8,128)}) custom-call(f32[2,8,1024,128]{3,2,1,0:T(8,128)S(1)} %get-tuple-element.19.aall, f32[2,8,1024,128]{3,2,1,0:T(8,128)S(1)} %get-tuple-element.20.pall, ...), custom_call_target="tpu_custom_call" | custom-call | tf_op jit(solution)/shard_map/grads/pallas_call | solution.py:395

commit v6 on v5

--- a/solution.py
+++ b/solution.py
@@ -27,13 +27,14 @@
     z1_hbm, z2_hbm, c_hbm, q1_hbm, q2_hbm,
     aall, pall, rinv, zt, cpad, small, lse_sum,
     xbuf, zall, sall, atr, cpart, csum,
-    in_sem, send_sem, recv_sem, zsend_sem, zrecv_sem,
+    sem, recv_sem, zrecv_sem,
 ):
     tiles = cpad.shape[0] // LANES
     rows = batch + queue
     total_rows = n * rows
     coef = 1.0 / (2 * n * batch * TEMPERATURE)
     scale10 = math.log2(math.e) / TEMPERATURE
+    scale20 = math.log2(math.e) / EPSILON
 
     me = lax.axis_index("data")
     bit0 = lax.rem(me, 2)
@@ -46,23 +47,23 @@
 
     far_first = (6, 7, 4, 5, 2, 3, 1)
 
-    c_in = pltpu.make_async_copy(c_hbm, cpad.at[pl.ds(0, protos)], in_sem.at[2])
+    barrier = pltpu.get_barrier_semaphore()
+    for k in far_first:
+        pl.semaphore_signal(barrier, inc=1, device_id=(peer(k),), device_id_type=MESH)
+
+    c_in = pltpu.make_async_copy(c_hbm, cpad.at[pl.ds(0, protos)], sem.at[2])
 
     def rows_in(v):
         z_hbm, q_hbm = ((z1_hbm, q1_hbm), (z2_hbm, q2_hbm))[v]
-        pltpu.make_async_copy(z_hbm, xbuf.at[v, pl.ds(0, batch)], in_sem.at[v]).start()
-        pltpu.make_async_copy(q_hbm, xbuf.at[v, pl.ds(batch, queue)], in_sem.at[v]).start()
+        pltpu.make_async_copy(z_hbm, xbuf.at[v, pl.ds(0, batch)], sem.at[v]).start()
+        pltpu.make_async_copy(q_hbm, xbuf.at[v, pl.ds(batch, queue)], sem.at[v]).start()
 
     def wait_rows(v):
-        pltpu.make_async_copy(xbuf.at[v], xbuf.at[v], in_sem.at[v]).wait()
+        pltpu.make_async_copy(xbuf.at[v], xbuf.at[v], sem.at[v]).wait()
 
     c_in.start()
     rows_in(0)
     rows_in(1)
-
-    barrier = pltpu.get_barrier_semaphore()
-    for k in far_first:
-        pl.semaphore_signal(barrier, inc=1, device_id=(peer(k),), device_id_type=MESH)
 
     cpad[pl.ds(protos, cpad.shape[0] - protos), :] = jnp.zeros((cpad.shape[0] - protos, LANES), BF16)
     c_in.wait()
@@ -82,7 +83,7 @@
     def sum_copy(t, v, k, slots):
         return pltpu.make_async_remote_copy(
             src_ref=csum.at[t, v, slots], dst_ref=csum.at[t, v, slots],
-            send_sem=send_sem.at[v], recv_sem=recv_sem.at[t, v],
+            send_sem=sem.at[v], recv_sem=recv_sem.at[t % 2, v],
             device_id=(peer(k),), device_id_type=MESH)
 
     def all_sums(t, v):
@@ -111,8 +112,7 @@
             for jj in range(tiles // 2):
                 s = lax.dot_general(x, cpad[pl.ds(jj * 256, 256), :], NT, preferred_element_type=F32)
                 for h in range(2):
-                    e = jnp.exp2(s[:, h * LANES:(h + 1) * LANES] * scale10)
-                    a = e * e
+                    a = jnp.exp2(s[:, h * LANES:(h + 1) * LANES] * scale20)
                     atr[v, 2 * jj + h, pl.ds(start, size), :] = a
                     acc[2 * jj + h] = acc[2 * jj + h] + fold(a)
         return acc
@@ -140,25 +140,28 @@
 
     def z_copy(k, target, src, dst):
         return pltpu.make_async_remote_copy(
-            src_ref=src, dst_ref=dst, send_sem=zsend_sem.at[0], recv_sem=zrecv_sem.at[k - 1],
+            src_ref=src, dst_ref=dst, send_sem=sem.at[2], recv_sem=zrecv_sem.at[(0, 1, 2, 3)[k // 2] if k in (1, 2, 4, 6) else 4],
             device_id=(peer(target),), device_id_type=MESH)
 
-    for k in (6, 2, 4, 1):
+    for k in (1, 2, 4, 6):
         for v in range(2):
             z_copy(k, k, xbuf.at[v, pl.ds(0, batch)], zall.at[me, v]).start()
 
     def z_arrived(k):
         z_copy(k, k, zall.at[peer(k)], zall.at[peer(k)]).wait_recv()
+
+    def relays_arrived(k):
+        z_copy(3, 1, zall.at[pl.ds(0, 3)], zall.at[pl.ds(0, 3)]).wait_recv()
 
     def relay(k):
         z_arrived(k)
         z_copy(k + 1, 1, zall.at[peer(k)], zall.at[peer(k)]).start()
 
-    def prepare(k):
+    def block_of(k):
+        return pl.ds(pl.multiple_of(peer(k) * batch, batch), batch)
+
+    def transport(k):
         d = peer(k)
-        if k in (3, 5, 7, 1):
-            z_arrived(k)
-        sl = pl.ds(pl.multiple_of(d * batch, batch), batch)
         z = [xbuf[v, pl.ds(0, batch), :] if k == 0 else zall[d, v] for v in range(2)]
         for v in range(2):
             zt[:, pl.ds(pl.multiple_of((v * n + d) * batch, batch), batch)] = z[v].astype(F32).T
@@ -175,35 +178,45 @@
                 a = e * e
                 for v in range(2):
                     half = slice(v * batch, (v + 1) * batch)
-                    aall[v, j, sl, :] = a[half]
-                    pall[v, j, sl, :] = e[half]
-                    sall[v, j, sl, :] = sj[half]
+                    aall[v, j, block_of(k), :] = a[half]
+                    pall[v, j, block_of(k), :] = e[half]
+                    sall[v, j, block_of(k), :] = sj[half]
                 p = e if p is None else p + e
-        r = jnp.sum(p, axis=1, keepdims=True)
+        return jnp.sum(p, axis=1, keepdims=True)
+
+    def softmax(k, r):
+        lse_sum[peer(k)] = fold(jnp.broadcast_to(jnp.log(r), (2 * batch, LANES)))
         inv = coef / r
-        lse_sum[d] = fold(jnp.broadcast_to(jnp.log(r), (2 * batch, LANES)))
         for v in range(2):
             for j in range(tiles):
-                pall[v, j, sl, :] = pall[v, j, sl, :] * inv[v * batch:(v + 1) * batch]
-
-    prepare(0)
+                pall[v, j, block_of(k), :] = pall[v, j, block_of(k), :] * inv[v * batch:(v + 1) * batch]
+
+    def prepare(steps):
+        last = None
+        for k, before in steps:
+            before(k)
+            r = transport(k)
+            if last is not None:
+                softmax(*last)
+            last = k, r
+        softmax(*last)
+
+    def ready(k):
+        pass
+
+    prepare([(0, ready), (1, z_arrived)])
     for v in range(2):
         col_scale(0, v)
         publish(1, v, sink_pass(v))
         send_sums(1, v)
 
-    prepare(1)
-    for k in (2, 4, 6):
-        relay(k)
-    for k in (2, 4):
-        prepare(k)
+    prepare([(2, relay), (4, relay)])
+    relay(6)
     for v in range(2):
         col_scale(1, v)
         publish(2, v, sink_pass(v))
         send_sums(2, v)
-    for k in (6, 3, 5, 7):
-        prepare(k)
-
+    prepare([(6, ready), (3, relays_arrived), (5, ready), (7, ready)])
 
     def row_scale(v):
         w = [small[v, j:j + 1, :] for j in range(tiles)]
@@ -383,10 +396,8 @@
                 pltpu.VMEM((2, 8 * tiles, LANES), F32),
                 pltpu.VMEM((ROUNDS, 2, n, tiles, LANES), F32),
                 sem((3,)),
-                sem((2,)),
-                sem((ROUNDS, 2)),
-                sem((1,)),
-                sem((n - 1,)),
+                sem((2, 2)),
+                sem((5,)),
             ],
             compiler_params=pltpu.CompilerParams(
                 collective_id=0, has_side_effects=True, vmem_limit_bytes=20 << 20),

time: 19.1 us -> 19.1 us (level)
  no operation moved by 1% of the time
where the time goes in v6:
time: 19.1 us; the launch traced here: 19 us
  Pallas kernels  18.3 us (96%)
  between operations  0.64 us (3%)
    pallas_call x1, Pallas kernels, local_step(): pl.pallas_call(functools.partial(sums_kernel, n, k, batch, queue), out_sh...  16.1 us
    pallas_call x1, Pallas kernels, local_step(): pl.pallas_call(functools.partial(grads_kernel, n, k, batch), out_shape=(j...  2.25 us

profile of v6, /device:TPU:0, one launch (start us, length us, event | category | flops | bytes accessed | tf_op | source)
XLA Modules:
  0.0 19.0 jit_solution(7416645331933928710)
XLA Ops:
  0.6 16.1 %sums.1 = (f32[2,8,1024,128]{3,2,1,0:T(8,128)S(1)}, f32[2,8,1024,128]{3,2,1,0:T(8,128)S(1)}, f32[2,1024,128]{2,1,0:T(8,128)S(1)}, f32[128,2048]{1,0:T(8,128)S(1)...) custom-call(bf16[128,128]{1,0:T(8,128)(2,1)} %z1_hbm.1, ...), custom_call_target="tpu_custom_call" | custom-call | tf_op jit(solution)/shard_map/sums/pallas_call | solution.py:378
  16.7 2.3 %grads.1 = (f32[1000,128]{1,0:T(8,128)}, f32[1000,128]{1,0:T(8,128)}, f32[1,1]{1,0:T(1,128)}, f32[128,128]{1,0:T(8,128)}, f32[128,128]{1,0:T(8,128)}, /*index=5*/f32[1000,128]{1,0:T(8,128)}) custom-call(f32[2,8,1024,128]{3,2,1,0:T(8,128)S(1)} %get-tuple-element.19.aall, f32[2,8,1024,128]{3,2,1,0:T(8,128)S(1)} %get-tuple-element.20.pall, ...), custom_call_target="tpu_custom_call" | custom-call | tf_op jit(solution)/shard_map/grads/pallas_call | solution.py:406

commit v7 on v6

--- a/solution.py
+++ b/solution.py
@@ -27,7 +27,7 @@
     z1_hbm, z2_hbm, c_hbm, q1_hbm, q2_hbm,
     aall, pall, rinv, zt, cpad, small, lse_sum,
     xbuf, zall, sall, atr, cpart, csum,
-    sem, recv_sem, zrecv_sem,
+    sem, recv_sem, zrecv_sem, xrecv_sem,
 ):
     tiles = cpad.shape[0] // LANES
     rows = batch + queue
@@ -40,6 +40,10 @@
     bit0 = lax.rem(me, 2)
     bit1 = lax.rem(me // 2, 2)
     bit2 = me // 4
+    chip = me // 2
+    chips = n // 2
+    odd = bit0 == 1
+    even = bit0 == 0
 
     def peer(k):
         b0, b1, b2 = k % 2, (k // 2) % 2, k // 4
@@ -55,11 +59,11 @@
 
     def rows_in(v):
         z_hbm, q_hbm = ((z1_hbm, q1_hbm), (z2_hbm, q2_hbm))[v]
-        pltpu.make_async_copy(z_hbm, xbuf.at[v, pl.ds(0, batch)], sem.at[v]).start()
-        pltpu.make_async_copy(q_hbm, xbuf.at[v, pl.ds(batch, queue)], sem.at[v]).start()
+        pltpu.make_async_copy(z_hbm, xbuf.at[0, v, pl.ds(0, batch)], sem.at[v]).start()
+        pltpu.make_async_copy(q_hbm, xbuf.at[0, v, pl.ds(batch, queue)], sem.at[v]).start()
 
     def wait_rows(v):
-        pltpu.make_async_copy(xbuf.at[v], xbuf.at[v], sem.at[v]).wait()
+        pltpu.make_async_copy(xbuf.at[0, v], xbuf.at[0, v], sem.at[v]).wait()
 
     c_in.start()
     rows_in(0)
@@ -72,13 +76,13 @@
     tail_ok = lane < (protos - (tiles - 1) * LANES)
     tail_mask = tail_ok.astype(F32)
 
-    def publish(t, v, acc):
+    def publish(t, v, acc, slot):
         for j in range(tiles):
             cpart[v, pl.ds(8 * j, 8), :] = acc[j]
         out = cpart[v, pl.ds(0, tiles, stride=8), :]
         for s in range(1, 8):
             out = out + cpart[v, pl.ds(s, tiles, stride=8), :]
-        csum[t, v, me] = out
+        csum[t, v, slot] = out
 
     def sum_copy(t, v, k, slots):
         return pltpu.make_async_remote_copy(
@@ -86,41 +90,39 @@
             send_sem=sem.at[v], recv_sem=recv_sem.at[t % 2, v],
             device_id=(peer(k),), device_id_type=MESH)
 
-    def all_sums(t, v):
-        return sum_copy(t, v, 1, pl.ds(0, n - 1))
-
-    def send_sums(t, v):
-        if t > 0:
-            all_sums(t, v).wait_send()
-        for k in far_first:
-            sum_copy(t, v, k, me).start()
-
-    def col_scale(t, v):
-        all_sums(t, v).wait_recv()
+    def sums(t, v, count):
+        return sum_copy(t, v, 1, pl.ds(0, count))
+
+    def send_sums(t, v, slot, peers):
+        for k in peers:
+            sum_copy(t, v, k, slot).start()
+
+    def col_scale(t, v, slots):
         c = csum[t, v, 0]
-        for d in range(1, n):
+        for d in range(1, slots):
             c = c + csum[t, v, d]
         w = 1.0 / (protos * c)
         index = (lax.broadcasted_iota(jnp.int32, (tiles, LANES), 0) * LANES
                  + lax.broadcasted_iota(jnp.int32, (tiles, LANES), 1))
         small[v] = jnp.where(index < protos, w, 0.0)
 
-    def first_pass(v):
+    def first_pass(v, source, base):
         acc = [jnp.zeros((8, LANES), F32) for _ in range(tiles)]
         for start, size in ((0, rows // 2), (rows // 2, rows // 2)):
-            x = xbuf[v, pl.ds(start, size), :]
+            x = xbuf[source, v, pl.ds(start, size), :]
             for jj in range(tiles // 2):
                 s = lax.dot_general(x, cpad[pl.ds(jj * 256, 256), :], NT, preferred_element_type=F32)
                 for h in range(2):
                     a = jnp.exp2(s[:, h * LANES:(h + 1) * LANES] * scale20)
-                    atr[v, 2 * jj + h, pl.ds(start, size), :] = a
-                    acc[2 * jj + h] = acc[2 * jj + h] + fold(a)
+                    atr[v, 2 * jj + h, pl.ds(base + start, size), :] = a
+                    if base == 0:
+                        acc[2 * jj + h] = acc[2 * jj + h] + fold(a)
         return acc
 
     def sink_pass(v):
         acc = [jnp.zeros((8, LANES), F32) for _ in range(tiles)]
         step = 128
-        for b in range(rows // step):
+        for b in range(2 * rows // step):
             sl = pl.ds(b * step, step)
             p = atr[v, 0, sl, :] * small[v, 0:1, :]
             for j in range(1, tiles):
@@ -130,13 +132,28 @@
                 acc[j] = acc[j] + fold(atr[v, j, sl, :] * u)
         return acc
 
+    def x_copy(v):
+        return pltpu.make_async_remote_copy(
+            src_ref=xbuf.at[0, v], dst_ref=xbuf.at[1, v], send_sem=sem.at[3], recv_sem=xrecv_sem.at[v],
+            device_id=(peer(1),), device_id_type=MESH)
+
+    def first_round(v):
+        @pl.when(odd)
+        def _():
+            send_sums(0, v, me, (6, 4, 2))
+
+        @pl.when(even)
+        def _():
+            send_sums(0, v, me, (7, 5, 3, 1))
+            x_copy(v).start()
+
     wait_rows(0)
-    publish(0, 0, first_pass(0))
+    publish(0, 0, first_pass(0, 0, 0), me)
     pl.semaphore_wait(barrier, n - 1)
-    send_sums(0, 0)
+    first_round(0)
     wait_rows(1)
-    publish(0, 1, first_pass(1))
-    send_sums(0, 1)
+    publish(0, 1, first_pass(1, 0, 0), me)
+    first_round(1)
 
     def z_copy(k, target, src, dst):
         return pltpu.make_async_remote_copy(
@@ -145,7 +162,7 @@
 
     for k in (1, 2, 4, 6):
         for v in range(2):
-            z_copy(k, k, xbuf.at[v, pl.ds(0, batch)], zall.at[me, v]).start()
+            z_copy(k, k, xbuf.at[0, v, pl.ds(0, batch)], zall.at[me, v]).start()
 
     def z_arrived(k):
         z_copy(k, k, zall.at[peer(k)], zall.at[peer(k)]).wait_recv()
@@ -162,7 +179,7 @@
 
     def transport(k):
         d = peer(k)
-        z = [xbuf[v, pl.ds(0, batch), :] if k == 0 else zall[d, v] for v in range(2)]
+        z = [xbuf[0, v, pl.ds(0, batch), :] if k == 0 else zall[d, v] for v in range(2)]
         for v in range(2):
             zt[:, pl.ds(pl.multiple_of((v * n + d) * batch, batch), batch)] = z[v].astype(F32).T
         x = jnp.concatenate(z, axis=0)
@@ -204,19 +221,33 @@
     def ready(k):
         pass
 
-    prepare([(0, ready), (1, z_arrived)])
-    for v in range(2):
-        col_scale(0, v)
-        publish(1, v, sink_pass(v))
-        send_sums(1, v)
-
-    prepare([(2, relay), (4, relay)])
-    relay(6)
-    for v in range(2):
-        col_scale(1, v)
-        publish(2, v, sink_pass(v))
-        send_sums(2, v)
-    prepare([(6, ready), (3, relays_arrived), (5, ready), (7, ready)])
+    @pl.when(odd)
+    def _():
+        prepare([(0, ready)])
+        for v in range(2):
+            x_copy(v).wait_recv()
+            first_pass(v, 1, rows)
+        for v in range(2):
+            sums(0, v, n - 1).wait_recv()
+            col_scale(0, v, n)
+            sums(0, v, 3).wait_send()
+            publish(1, v, sink_pass(v), chip)
+            send_sums(1, v, chip, (6, 4, 2))
+        prepare([(1, z_arrived), (2, relay), (4, relay)])
+        relay(6)
+        for v in range(2):
+            sums(1, v, chips - 1).wait_recv()
+            col_scale(1, v, chips)
+            sums(1, v, chips - 1).wait_send()
+            publish(2, v, sink_pass(v), chip)
+            send_sums(2, v, chip, (7, 5, 3, 6, 4, 2, 1))
+        prepare([(6, ready), (3, relays_arrived), (5, ready), (7, ready)])
+
+    @pl.when(even)
+    def _():
+        prepare([(0, ready), (1, z_arrived), (2, relay), (4, relay)])
+        relay(6)
+        prepare([(6, ready), (3, relays_arrived), (5, ready), (7, ready)])
 
     def row_scale(v):
         w = [small[v, j:j + 1, :] for j in range(tiles)]
@@ -247,13 +278,35 @@
             last = this
         return part + scale(n - 1, *last)
 
-    col_scale(2, 0)
+    def last_scale(v):
+        @pl.when(odd)
+        def _():
+            sums(2, v, chips - 1).wait_recv()
+
+        @pl.when(even)
+        def _():
+            sums(2, v, chips).wait_recv()
+
+        col_scale(2, v, chips)
+
+    last_scale(0)
     part = row_scale(0)
-    col_scale(2, 1)
+    last_scale(1)
     small[2] = part + row_scale(1)
 
-    for v in range(2):
-        all_sums(2, v).wait_send()
+    @pl.when(odd)
+    def _():
+        for v in range(2):
+            sums(2, v, n - 1).wait_send()
+
+    @pl.when(even)
+    def _():
+        for v in range(2):
+            sums(0, v, 4).wait_send()
+        pltpu.make_async_remote_copy(
+            src_ref=xbuf.at[0], dst_ref=xbuf.at[1], send_sem=sem.at[3], recv_sem=xrecv_sem.at[0],
+            device_id=(peer(1),), device_id_type=MESH).wait_send()
+
     z_copy(1, 1, zall.at[pl.ds(0, n - 1)], zall.at[pl.ds(0, n - 1)]).wait_send()
 
 
@@ -389,18 +442,19 @@
             in_specs=[anywhere] * 5,
             out_specs=(vmem,) * 7,
             scratch_shapes=[
-                pltpu.VMEM((2, rows, width), BF16),
+                pltpu.VMEM((2, 2, rows, width), BF16),
                 pltpu.VMEM((n, 2, batch, width), BF16),
                 pltpu.VMEM((2, tiles, whole, LANES), F32),
-                pltpu.VMEM((2, tiles, rows, LANES), F32),
+                pltpu.VMEM((2, tiles, 2 * rows, LANES), F32),
                 pltpu.VMEM((2, 8 * tiles, LANES), F32),
                 pltpu.VMEM((ROUNDS, 2, n, tiles, LANES), F32),
-                sem((3,)),
+                sem((4,)),
                 sem((2, 2)),
                 sem((5,)),
+                sem((2,)),
             ],
             compiler_params=pltpu.CompilerParams(
-                collective_id=0, has_side_effects=True, vmem_limit_bytes=20 << 20),
+                collective_id=0, has_side_effects=True, vmem_limit_bytes=26 << 20),
             name="sums",
         )(*(pltpu.with_memory_space_constraint(x, pltpu.HBM) for x in (z_one, z_two, protos, queue_one, queue_two)))
         codes_one, codes_two, loss, dz_one, dz_two, grad_protos = pl.pallas_call(

time: 19.1 us -> 18.6 us (0.974)
  Pallas kernels: 18.3 us -> 17.7 us
    pallas_call x1, Pallas kernels: 16.1 us -> 15.4 us  [local_step(): pl.pallas_call(functools.partial(sums_kernel, n, k, batch, queue), out_sh...]
where the time goes in v7:
time: 18.6 us; the launch traced here: 18.5 us
  Pallas kernels  17.7 us (95%)
  between operations  0.8 us (4%)
    pallas_call x1, Pallas kernels, local_step(): pl.pallas_call(functools.partial(sums_kernel, n, k, batch, queue), out_sh...  15.4 us
    pallas_call x1, Pallas kernels, local_step(): pl.pallas_call(functools.partial(grads_kernel, n, k, batch), out_shape=(j...  2.25 us

profile of v7, /device:TPU:0, one launch (start us, length us, event | category | flops | bytes accessed | tf_op | source)
XLA Modules:
  0.0 18.5 jit_solution(16262646725246599271)
XLA Ops:
  0.6 15.4 %sums.1 = (f32[2,8,1024,128]{3,2,1,0:T(8,128)S(1)}, f32[2,8,1024,128]{3,2,1,0:T(8,128)S(1)}, f32[2,1024,128]{2,1,0:T(8,128)S(1)}, f32[128,2048]{1,0:T(8,128)S(1)...) custom-call(bf16[128,128]{1,0:T(8,128)(2,1)} %z1_hbm.1, ...), custom_call_target="tpu_custom_call" | custom-call | tf_op jit(solution)/shard_map/sums/pallas_call | solution.py:431
  16.1 2.3 %grads.1 = (f32[1000,128]{1,0:T(8,128)}, f32[1000,128]{1,0:T(8,128)}, f32[1,1]{1,0:T(1,128)}, f32[128,128]{1,0:T(8,128)}, f32[128,128]{1,0:T(8,128)}, /*index=5*/f32[1000,128]{1,0:T(8,128)}) custom-call(f32[2,8,1024,128]{3,2,1,0:T(8,128)S(1)} %get-tuple-element.19.aall, f32[2,8,1024,128]{3,2,1,0:T(8,128)S(1)} %get-tuple-element.20.pall, ...), custom_call_target="tpu_custom_call" | custom-call | tf_op jit(solution)/shard_map/grads/pallas_call | solution.py:460

commit v8 on v7

--- a/solution.py
+++ b/solution.py
@@ -52,9 +52,6 @@
     far_first = (6, 7, 4, 5, 2, 3, 1)
 
     barrier = pltpu.get_barrier_semaphore()
-    for k in far_first:
-        pl.semaphore_signal(barrier, inc=1, device_id=(peer(k),), device_id_type=MESH)
-
     c_in = pltpu.make_async_copy(c_hbm, cpad.at[pl.ds(0, protos)], sem.at[2])
 
     def rows_in(v):
@@ -67,6 +64,8 @@
 
     c_in.start()
     rows_in(0)
+    for k in far_first:
+        pl.semaphore_signal(barrier, inc=1, device_id=(peer(k),), device_id_type=MESH)
     rows_in(1)
 
     cpad[pl.ds(protos, cpad.shape[0] - protos), :] = jnp.zeros((cpad.shape[0] - protos, LANES), BF16)
@@ -157,22 +156,44 @@
 
     def z_copy(k, target, src, dst):
         return pltpu.make_async_remote_copy(
-            src_ref=src, dst_ref=dst, send_sem=sem.at[2], recv_sem=zrecv_sem.at[(0, 1, 2, 3)[k // 2] if k in (1, 2, 4, 6) else 4],
+            src_ref=src, dst_ref=dst, send_sem=sem.at[2], recv_sem=zrecv_sem.at[(0, 0, 1, 4, 2, 4, 3, 3)[k]],
             device_id=(peer(target),), device_id_type=MESH)
 
-    for k in (1, 2, 4, 6):
+    def z_send(k):
         for v in range(2):
             z_copy(k, k, xbuf.at[0, v, pl.ds(0, batch)], zall.at[me, v]).start()
 
-    def z_arrived(k):
-        z_copy(k, k, zall.at[peer(k)], zall.at[peer(k)]).wait_recv()
-
-    def relays_arrived(k):
-        z_copy(3, 1, zall.at[pl.ds(0, 3)], zall.at[pl.ds(0, 3)]).wait_recv()
+    def z_pass(k, owner, target):
+        z_copy(k, target, zall.at[peer(owner)], zall.at[peer(owner)]).start()
+
+    def z_arrived(k, count=1):
+        z_copy(k, 1, zall.at[pl.ds(0, count)], zall.at[pl.ds(0, count)]).wait_recv()
 
     def relay(k):
         z_arrived(k)
-        z_copy(k + 1, 1, zall.at[peer(k)], zall.at[peer(k)]).start()
+        z_pass(k + 1, k, 1)
+
+    def to_diagonal(k):
+        z_arrived(k)
+        z_pass(7, 1, 6)
+
+    def relay_diagonal(k):
+        z_arrived(6, 2)
+        z_pass(7, 6, 1)
+        z_pass(6, 7, 1)
+
+    def side_arrived(k):
+        z_arrived(3, 2)
+
+    def diagonal_arrived(k):
+        z_arrived(6, 2)
+
+    for k in (1, 2, 4):
+        z_send(k)
+
+    @pl.when(even)
+    def _():
+        z_send(6)
 
     def block_of(k):
         return pl.ds(pl.multiple_of(peer(k) * batch, batch), batch)
@@ -234,20 +255,18 @@
             publish(1, v, sink_pass(v), chip)
             send_sums(1, v, chip, (6, 4, 2))
         prepare([(1, z_arrived), (2, relay), (4, relay)])
-        relay(6)
         for v in range(2):
             sums(1, v, chips - 1).wait_recv()
             col_scale(1, v, chips)
             sums(1, v, chips - 1).wait_send()
             publish(2, v, sink_pass(v), chip)
             send_sums(2, v, chip, (7, 5, 3, 6, 4, 2, 1))
-        prepare([(6, ready), (3, relays_arrived), (5, ready), (7, ready)])
+        prepare([(3, side_arrived), (5, ready), (6, diagonal_arrived), (7, ready)])
 
     @pl.when(even)
     def _():
-        prepare([(0, ready), (1, z_arrived), (2, relay), (4, relay)])
-        relay(6)
-        prepare([(6, ready), (3, relays_arrived), (5, ready), (7, ready)])
+        prepare([(0, ready), (1, to_diagonal), (2, relay), (4, relay)])
+        prepare([(6, relay_diagonal), (7, ready), (3, side_arrived), (5, ready)])
 
     def row_scale(v):
         w = [small[v, j:j + 1, :] for j in range(tiles)]
@@ -289,6 +308,9 @@
 
         col_scale(2, v, chips)
 
+    def z_sent(count):
+        z_copy(1, 1, zall.at[pl.ds(0, count)], zall.at[pl.ds(0, count)]).wait_send()
+
     last_scale(0)
     part = row_scale(0)
     last_scale(1)
@@ -298,6 +320,7 @@
     def _():
         for v in range(2):
             sums(2, v, n - 1).wait_send()
+        z_sent(5)
 
     @pl.when(even)
     def _():
@@ -306,8 +329,8 @@
         pltpu.make_async_remote_copy(
             src_ref=xbuf.at[0], dst_ref=xbuf.at[1], send_sem=sem.at[3], recv_sem=xrecv_sem.at[0],
             device_id=(peer(1),), device_id_type=MESH).wait_send()
-
-    z_copy(1, 1, zall.at[pl.ds(0, n - 1)], zall.at[pl.ds(0, n - 1)]).wait_send()
+        z_sent(n)
+        z_sent(1)
 
 
 def grads_kernel(

time: 18.6 us -> 18.4 us (0.989)
  Pallas kernels: 17.7 us -> 17.4 us
    pallas_call x1, Pallas kernels: 15.4 us -> 15.2 us  [local_step(): pl.pallas_call(functools.partial(sums_kernel, n, k, batch, queue), out_sh...]
where the time goes in v8:
time: 18.4 us; the launch traced here: 18.2 us
  Pallas kernels  17.4 us (95%)
  between operations  0.8 us (4%)
    pallas_call x1, Pallas kernels, local_step(): pl.pallas_call(functools.partial(sums_kernel, n, k, batch, queue), out_sh...  15.2 us
    pallas_call x1, Pallas kernels, local_step(): pl.pallas_call(functools.partial(grads_kernel, n, k, batch), out_shape=(j...  2.25 us

profile of v8, /device:TPU:0, one launch (start us, length us, event | category | flops | bytes accessed | tf_op | source)
XLA Modules:
  0.0 18.2 jit_solution(16747727073786248594)
XLA Ops:
  0.6 15.2 %sums.1 = (f32[2,8,1024,128]{3,2,1,0:T(8,128)S(1)}, f32[2,8,1024,128]{3,2,1,0:T(8,128)S(1)}, f32[2,1024,128]{2,1,0:T(8,128)S(1)}, f32[128,2048]{1,0:T(8,128)S(1)...) custom-call(bf16[128,128]{1,0:T(8,128)(2,1)} %z1_hbm.1, ...), custom_call_target="tpu_custom_call" | custom-call | tf_op jit(solution)/shard_map/sums/pallas_call | solution.py:454
  15.8 2.3 %grads.1 = (f32[1000,128]{1,0:T(8,128)}, f32[1000,128]{1,0:T(8,128)}, f32[1,1]{1,0:T(1,128)}, f32[128,128]{1,0:T(8,128)}, f32[128,128]{1,0:T(8,128)}, /*index=5*/f32[1000,128]{1,0:T(8,128)}) custom-call(f32[2,8,1024,128]{3,2,1,0:T(8,128)S(1)} %get-tuple-element.19.aall, f32[2,8,1024,128]{3,2,1,0:T(8,128)S(1)} %get-tuple-element.20.pall, ...), custom_call_target="tpu_custom_call" | custom-call | tf_op jit(solution)/shard_map/grads/pallas_call | solution.py:483
